TPU v7x, 32 devices: a whole 2x2x4 slice. The times are simulated.
32 devices in a mesh: data: 2 (over x), outer: 4 (over z), expert: 4 (over y, core).
Axes of the slice: x: 2, y: 2, z: 4, core: 2. Of those that a mesh axis runs over, the one named last changes fastest.
Arguments:
- tokens: bfloat16 [2048, 2048], P(('data', 'outer', 'expert')), parts along dimension 0
- w_router: bfloat16 [2048, 64], replicated
- routes: int32 [2048, 8], P(('data', 'outer', 'expert')), parts along dimension 0
- w_gate: bfloat16 [64, 2048, 1024], P(('outer', 'expert'))
- w_up: bfloat16 [64, 2048, 1024], P(('outer', 'expert'))
- w_down: bfloat16 [64, 1024, 2048], P(('outer', 'expert'))
Outputs:
- output: bfloat16 [2048, 2048], P(('data', 'outer', 'expert')), parts along dimension 0
There are 2 independent parts. A program takes and returns all parts, laid end to end along the dimension named above; an argument that names none is the same for every part.
All inputs are finite; a program needn't handle non-finite values.
Results may differ from a plain program's by a relative error of at most 0.00127.
Values are sent between devices in bfloat16 or wider.
A program may use at most 1 GiB of HBM per device.

v0:
```python
import jax
import jax.numpy as jnp
from jax import lax
from jax.sharding import PartitionSpec as P


def local_routes(tokens, w_router, routes, num_dev, capacity):
    tok_count, top_k = routes.shape
    num_exp = w_router.shape[1]
    per_dev = num_exp // num_dev
    logits = jnp.dot(tokens, w_router, preferred_element_type=jnp.float32)
    gate_vals = jax.nn.softmax(jnp.take_along_axis(logits, routes, axis=1), axis=-1)
    flat_ids = routes.reshape(-1)
    onehot = (flat_ids[:, None] == jnp.arange(num_exp)[None, :]).astype(jnp.int32)
    slot_pos = jnp.sum((jnp.cumsum(onehot, axis=0) - onehot) * onehot, axis=1)
    total_slots = num_exp * capacity
    send_pos = (flat_ids % per_dev) * (num_dev * capacity) + (flat_ids // per_dev) * capacity + slot_pos
    dest_slot = jnp.where(slot_pos < capacity, send_pos, total_slots)
    pair_tok = jnp.arange(tok_count * top_k, dtype=jnp.int32) // top_k
    slot_tok = jnp.full((total_slots,), tok_count, jnp.int32).at[dest_slot].set(pair_tok, mode='drop')
    return gate_vals, dest_slot, slot_tok


def expert_ffn(expert_in, w_gate, w_up, w_down):
    gate_act = jnp.einsum('erd,edf->erf', expert_in, w_gate, preferred_element_type=jnp.float32)
    up_lin = jnp.einsum('erd,edf->erf', expert_in, w_up, preferred_element_type=jnp.float32)
    hidden = (jax.nn.silu(gate_act) * up_lin).astype(jnp.bfloat16)
    return jnp.einsum('erf,efd->erd', hidden, w_down, preferred_element_type=jnp.float32).astype(jnp.bfloat16)


def solution(mesh):
    outer_size = mesh.shape['outer']
    group_size = mesh.shape['expert']
    num_dev = outer_size * group_size
    row_spec = P(('data', 'outer', 'expert'), None)
    weight_spec = P(('outer', 'expert'), None, None)

    def per_device(tokens, w_router, routes, w_gate, w_up, w_down):
        tok_count, top_k = routes.shape
        model_dim = tokens.shape[1]
        num_exp = w_router.shape[1]
        per_dev = w_gate.shape[0]
        capacity = (5 * tok_count * top_k + 4 * num_exp - 1) // (4 * num_exp)
        gate_vals, dest_slot, slot_tok = local_routes(tokens, w_router, routes, num_dev, capacity)
        send_buf = jnp.take(tokens, slot_tok, axis=0, mode='fill', fill_value=0)
        send_buf = send_buf.reshape(per_dev, outer_size, group_size, capacity, model_dim)
        recv_buf = lax.all_to_all(send_buf, 'outer', 1, 1, tiled=True)
        recv_buf = lax.all_to_all(recv_buf, 'expert', 2, 2, tiled=True)
        expert_out = expert_ffn(recv_buf.reshape(per_dev, num_dev * capacity, model_dim), w_gate, w_up, w_down)
        back_buf = expert_out.reshape(per_dev, outer_size, group_size, capacity, model_dim)
        back_buf = lax.all_to_all(back_buf, 'expert', 2, 2, tiled=True)
        back_buf = lax.all_to_all(back_buf, 'outer', 1, 1, tiled=True)
        picked = jnp.take(back_buf.reshape(num_exp * capacity, model_dim), dest_slot, axis=0, mode='fill', fill_value=0)
        weighted = gate_vals[:, :, None] * picked.reshape(tok_count, top_k, model_dim).astype(jnp.float32)
        return jnp.sum(weighted, axis=1).astype(jnp.bfloat16)

    return jax.shard_map(per_device, mesh=mesh, in_specs=(row_spec, P(), row_spec, weight_spec, weight_spec, weight_spec), out_specs=row_spec, check_vma=False)
```

profile of v0, /device:TPU:0, one launch (start us, length us, event | category | flops | bytes accessed | tf_op | source)
XLA Modules:
  0.0 264.3 jit_solution(10554808408947091142)
XLA Ops:
  0.0 0.8 copy.66
  1.1 1.2 reduce-window.6
  2.8 2.4 scatter_custom_fusion
  5.3 3.4 %gather_fusion = bf16[640,2048]{1,0:T(8,128)(2,1)S(1)} fusion(bf16[64,2048]{1,0:T(8,128)(2,1)S(1)} %copy-done, s32[1024]{0:T(1024)S(1)} %pad_clamp_fusion.1), kind=kCustom, calls=%fused_computation | custom fusion | bytes 5245440 | tf_op jit(solution)/shard_map/jit(_take)/gather | solution.py:45
  8.7 2.8 %gather.18 = bf16[4,4,4,10,2048]{4,3,2,1,0:T(8,128)(2,1)} reshape(bf16[640,2048]{1,0:T(8,128)(2,1)S(1)} %gather_fusion) | data formatting | bytes 5242880 | tf_op jit(solution)/shard_map/jit(_take)/gather | solution.py:45
  11.6 2.7 %broadcast_select_fusion = bf16[4,4,4,10,2048]{4,3,2,1,0:T(8,128)(2,1)S(1)} fusion(bf16[4,4,4,10,2048]{4,3,2,1,0:T(8,128)(2,1)} %gather.18, pred[4,4,4,10]{3,2,1,0:T(4,128)(4,1)S(1)} %broadcast_in_dim.47), kind=kLoop, calls=%fused_computation.5 | loop fusion | flops 1310720 | bytes 5243520 | tf_op jit(solution)/shard_map/jit(_take)/select_n | solution.py:45
  14.3 2.2 copy.73
  16.6 65.9 %all_to_all.20 = bf16[4,4,4,10,2048]{4,2,3,0,1:T(4,128)(2,1)S(1)} all-to-all(bf16[4,4,4,10,2048]{4,2,3,0,1:T(4,128)(2,1)S(1)} %copy.73), channel_id=1, replica_groups=mesh['data'=2,'outer'=4,'expert'=4] {'outer'}, dimensions={1} | all-to-all | bytes 5242880 | tf_op jit(solution)/shard_map/all_to_all | solution.py:47
  82.5 2.0 copy.74
  84.5 34.1 %all_to_all.21 = bf16[4,4,4,10,2048]{4,1,3,0,2:T(4,128)(2,1)S(1)} all-to-all(bf16[4,4,4,10,2048]{4,1,3,0,2:T(4,128)(2,1)S(1)} %copy.74), channel_id=1, replica_groups=mesh['data'=2,'outer'=4,'expert'=4] {'expert'}, dimensions={2} | all-to-all | bytes 5242880 | tf_op jit(solution)/shard_map/all_to_all | solution.py:48
  118.6 2.0 copy.75
  120.7 6.9 %fusion = f32[4,160,1024]{2,1,0:T(8,128)} fusion(bf16[4,2048,1024]{2,1,0:T(8,128)(2,1)S(1)} %bitcast.37, bf16[4,160,2048]{2,0,1:T(4,128)(2,1)S(1)} %bitcast.39), kind=kOutput, calls=%fused_computation.8 | convolution fusion | flops 2684354560 | bytes 22020096 | tf_op jit(solution)/shard_map/erd,edf->erf/dot_general | solution.py:26
  127.7 16.6 %convolution_convert_fusion = bf16[4,160,2048]{2,1,0:T(8,128)(2,1)} fusion(bf16[4,1024,2048]{2,1,0:T(8,128)(2,1)} %param.11, f32[4,160,1024]{2,1,0:T(8,128)} %fusion, bf16[4,2048,1024]{2,1,0:T(8,128)(2,1)} %param.9, bf16[4,160,2048]{2,0,1:T(4,128)(2,1)S(1)} %bitcast.40), kind=kOutput, calls=%fused_computation.6 | convolution fusion | flops 5373952000 | bytes 41418752 | tf_op jit(solution)/shard_map/erf,efd->erd/dot_general | solution.py:28
  144.2 3.8 %copy.78 = bf16[4,160,2048]{2,0,1:T(4,128)(2,1)S(1)} copy(bf16[4,160,2048]{2,1,0:T(8,128)(2,1)} %convolution_convert_fusion) | data formatting | bytes 5242880 | tf_op jit(solution)/shard_map/convert_element_type | solution.py:28
  148.0 1.3 copy.79
  149.3 33.8 %all_to_all.22 = bf16[4,4,4,10,2048]{4,0,3,1,2:T(4,128)(2,1)S(1)} all-to-all(bf16[4,4,4,10,2048]{4,0,3,1,2:T(4,128)(2,1)S(1)} %copy.79), channel_id=1, replica_groups=mesh['data'=2,'outer'=4,'expert'=4] {'expert'}, dimensions={2} | all-to-all | bytes 5242880 | tf_op jit(solution)/shard_map/all_to_all | solution.py:51
  183.0 2.8 %copy.80 = bf16[4,4,4,10,2048]{4,0,3,2,1:T(4,128)(2,1)} copy(bf16[4,4,4,10,2048]{4,0,3,1,2:T(4,128)(2,1)S(1)} %all_to_all.22) | data formatting | bytes 5242880 | tf_op jit(solution)/shard_map/all_to_all | solution.py:51
  185.8 3.8 %all-to-all-start.3 = ((bf16[4,4,4,10,2048]{4,0,3,2,1:T(4,128)(2,1)}), bf16[4,4,4,10,2048]{4,0,3,2,1:T(4,128)(2,1)S(1)}, u32[]{:S(2)}, u32[]{:S(2)}) async-start(bf16[4,4,4,10,2048]{4,0,3,2,1:T(4,128)(2,1)} %copy.80), calls=%async_computation.3 | async-start | bytes 5242880 | tf_op jit(solution)/shard_map/all_to_all | solution.py:52
  190.1 3.8 %gather_fusion.2 = f32[512]{0:T(512)S(1)} fusion(f32[64,64]{1,0:T(8,128)S(1)} %fusion.34, s32[512]{0:T(512)S(1)} %reshape.232), kind=kCustom, calls=%fused_computation.2 | custom fusion | bytes 8192 | tf_op jit(solution)/shard_map/jit(take_along_axis)/gather | solution.py:12
  194.4 54.2 %all-to-all-done.3 = bf16[4,4,4,10,2048]{4,0,3,2,1:T(4,128)(2,1)S(1)} async-done(((bf16[4,4,4,10,2048]{4,0,3,2,1:T(4,128)(2,1)}), bf16[4,4,4,10,2048]{4,0,3,2,1:T(4,128)(2,1)S(1)}, u32[]{:S(2)}, u32[]{:S(2)}) %all-to-all-start.3) | async-done | bytes 2621472 | tf_op jit(solution)/shard_map/all_to_all | solution.py:52
  248.7 3.5 %copy.81 = bf16[4,4,4,10,2048]{4,3,2,1,0:T(8,128)(2,1)} copy(bf16[4,4,4,10,2048]{4,0,3,2,1:T(4,128)(2,1)S(1)} %all-to-all-done.3) | data formatting | bytes 5242880 | tf_op jit(solution)/shard_map/all_to_all | solution.py:52
  252.2 4.1 %reshape.215 = bf16[640,2048]{1,0:T(8,128)(2,1)S(1)} reshape(bf16[4,4,4,10,2048]{4,3,2,1,0:T(8,128)(2,1)} %copy.81) | data formatting | bytes 5242880 | tf_op jit(solution)/shard_map/reshape | solution.py:53
  256.3 3.3 %gather_fusion.1 = bf16[512,2048]{1,0:T(8,128)(2,1)} fusion(bf16[640,2048]{1,0:T(8,128)(2,1)S(1)} %reshape.215, s32[1024]{0:T(1024)S(1)} %pad_clamp_fusion), kind=kCustom, calls=%fused_computation.1 | custom fusion | bytes 4196352 | tf_op jit(solution)/shard_map/jit(_take)/gather | solution.py:53
  259.6 4.7 %multiply_reduce_fusion = bf16[64,2048]{1,0:T(8,128)(2,1)} fusion(bf16[512,2048]{1,0:T(8,128)(2,1)} %gather_fusion.1, f32[64,8]{1,0:T(8,128)S(1)} %copy.65, pred[64,8]{1,0:T(8,128)(4,1)S(1)} %copy.71), kind=kLoop, calls=%fused_computation.4 | loop fusion | flops 4063232 | bytes 2361856 | tf_op jit(solution)/shard_map/reduce_sum | solution.py:55
  (44 shorter events, 1.9 us)
Async XLA Ops:
  0.0 5.3 %copy-start = (bf16[64,2048]{1,0:T(8,128)(2,1)S(1)}, bf16[64,2048]{1,0:T(8,128)(2,1)}, u32[]{:S(2)}) copy-start(bf16[64,2048]{1,0:T(8,128)(2,1)} %param.6) | copy-start | bytes 786436
  11.6 109.1 %slice-start = ((s8[16777216]{0:T(1024)(128)(4,1)}), s8[4194304]{0:T(1024)(128)(4,1)S(1)}, s32[]{:S(2)}) async-start(s8[16777216]{0:T(1024)(128)(4,1)} %bitcast.36), calls=%async_computation.4 | async-start | bytes 8388608
  14.3 106.4 %slice-start.1 = ((s8[16777216]{0:T(1024)(128)(4,1)}), s8[4194304]{0:T(1024)(128)(4,1)S(1)}, s32[]{:S(2)}) async-start(s8[16777216]{0:T(1024)(128)(4,1)} %bitcast.36), calls=%async_computation.5 | async-start | bytes 8388608
  16.6 104.1 %slice-start.2 = ((s8[16777216]{0:T(1024)(128)(4,1)}), s8[4194304]{0:T(1024)(128)(4,1)S(1)}, s32[]{:S(2)}) async-start(s8[16777216]{0:T(1024)(128)(4,1)} %bitcast.36), calls=%async_computation.6 | async-start | bytes 8388608
  84.5 36.2 %slice-start.3 = ((s8[16777216]{0:T(1024)(128)(4,1)}), s8[4194304]{0:T(1024)(128)(4,1)S(1)}, s32[]{:S(2)}) async-start(s8[16777216]{0:T(1024)(128)(4,1)} %bitcast.36), calls=%async_computation.7 | async-start | bytes 8388608
  185.8 3.9 %copy-start.2 = (s32[64,8]{0,1:T(8,128)S(1)}, s32[64,8]{0,1:T(8,128)}, u32[]{:S(2)}) copy-start(s32[64,8]{0,1:T(8,128)} %param.8) | copy-start | bytes 6148
  185.8 4.1 %copy-start.1 = (bf16[2048,64]{0,1:T(8,128)(2,1)S(1)}, bf16[2048,64]{0,1:T(8,128)(2,1)}, u32[]{:S(2)}) copy-start(bf16[2048,64]{0,1:T(8,128)(2,1)} %param.7) | copy-start | bytes 786436
  185.8 62.8 %all-to-all-start.3 = ((bf16[4,4,4,10,2048]{4,0,3,2,1:T(4,128)(2,1)}), bf16[4,4,4,10,2048]{4,0,3,2,1:T(4,128)(2,1)S(1)}, u32[]{:S(2)}, u32[]{:S(2)}) async-start(bf16[4,4,4,10,2048]{4,0,3,2,1:T(4,128)(2,1)} %copy.80), calls=%async_computation.3 | async-start | bytes 5242880 | tf_op jit(solution)/shard_map/all_to_all | solution.py:52
where the time goes:
time: 265 us; the launch traced here: 264 us
  blocking collectives  134 us (51%)
  waiting for transfers between devices  54.2 us (20%)
  local copies, waits for them, and re-layouts  39.6 us (15%)
  matrix products  23.7 us (9%)
  other arithmetic  8.89 us (3%)
  starting transfers between devices  3.78 us (1%)
    all_to_all x1, blocking collectives, per_device(): recv_buf = lax.all_to_all(send_buf, 'outer', 1, 1, tiled=True)  65.9 us
    all_to_all x1, waiting for transfers between devices, per_device(): back_buf = lax.all_to_all(back_buf, 'outer', 1, 1, tiled=True)  54.2 us
    all_to_all x1, blocking collectives, per_device(): recv_buf = lax.all_to_all(recv_buf, 'expert', 2, 2, tiled=True)  34.1 us
    all_to_all x1, blocking collectives, per_device(): back_buf = lax.all_to_all(back_buf, 'expert', 2, 2, tiled=True)  33.8 us
    dot_general x1, matrix products, expert_ffn(): jnp.einsum('erf,efd->erd', hidden, w_down, preferred_element_type=jnp.flo...  16.6 us
    dot_general x1, matrix products, expert_ffn(): jnp.einsum('erd,edf->erf', expert_in, w_up, preferred_element_type=jnp.fl...  6.93 us
    gather x2, local copies, waits for them, and re-layouts, per_device(): send_buf = jnp.take(tokens, slot_tok, axis=0, mode='fill', fill_value=0)  6.2 us
  transfers between devices with their start and end apart: 1, of which 1 were waited for; matrix products, arithmetic and copies ran while one was open for 2% of the time, Pallas kernels for 0%

commit v1 on v0

v1 whole, which is shorter than its diff:
```python
import functools

import jax
import jax.numpy as jnp
from jax import lax
from jax.experimental import pallas as pl
from jax.experimental.pallas import tpu as pltpu
from jax.sharding import PartitionSpec as P

MESH = pl.DeviceIdType.MESH
F32, BF16 = jnp.float32, jnp.bfloat16
PLANES = 4
COLS = 4
JLOC = 4
TOK = 64
TOPK = 8
CAP = 10
DIM = 2048
FF = 1024
NEXP = 64
CW = 512
NC = DIM // CW
SL = PLANES * CAP
ROWS = COLS * SL
CT = PLANES * TOK


def iota(shape, dim):
    return lax.broadcasted_iota(jnp.int32, shape, dim)


def dot(a, b):
    return jnp.dot(a, b, preferred_element_type=F32)


def dot_nt(a, b):
    return lax.dot_general(a, b, (((1,), (1,)), ((), ())), preferred_element_type=F32)


def dot_tn(a, b):
    return lax.dot_general(a, b, (((0,), (0,)), ((), ())), preferred_element_type=F32)


def kernel(x_hbm, wr_ref, rt_ref, wg_hbm, wu_hbm, wd_hbm, out_ref,
           x_all, r_all, xs, wgb, wub, wdb, hid, ysend, yrecv, wst, part, zr,
           lsem, wsem, dsem, bx_s, br_s, bx_r, br_r, ys_s, ys_r, zs_s, zs_r):
    d = lax.axis_index('data')
    o = lax.axis_index('outer')
    e = lax.axis_index('expert')
    c = e % 2
    y = e // 2
    mate = e + 1 - 2 * c
    yp = e + 2 - 4 * y
    diag = mate + yp - e
    rel = (e, mate, yp, diag)

    own = pl.ds(pl.multiple_of(o * TOK, TOK), TOK)
    xcp = pltpu.make_async_copy(x_hbm, x_all.at[e, own], lsem)
    xcp.start()
    wcp = []
    for j in range(JLOC):
        a = pltpu.make_async_copy(wg_hbm.at[j], wgb.at[j], wsem.at[0, j])
        b = pltpu.make_async_copy(wu_hbm.at[j], wub.at[j], wsem.at[1, j])
        a.start()
        b.start()
        wcp.append((a, b))

    def wd_copy(k):
        return pltpu.make_async_copy(
            wd_hbm.at[:, :, pl.ds(k * CW, CW)], wdb.at[k % 2], dsem.at[k % 2])

    wd_copy(0).start()
    wd_copy(1).start()

    dup = (iota((TOK, 128), 1) % TOK == iota((TOK, 128), 0)).astype(BF16)
    r_all[e, o] = dot_tn((rt_ref[...] + 1).astype(F32).astype(BF16), dup) - 1.0

    barrier = pltpu.get_barrier_semaphore()

    def greet(oo, ee):
        pl.semaphore_signal(barrier, inc=1, device_id=(d, oo, ee), device_id_type=MESH)

    for q in range(1, 4):
        greet(o, rel[q])

    @pl.when(o > 0)
    def _():
        greet(o - 1, e)

    @pl.when(o < PLANES - 1)
    def _():
        greet(o + 1, e)

    edge = (o == 0) | (o == PLANES - 1)

    @pl.when(edge)
    def _():
        pl.semaphore_wait(barrier, 4)

    @pl.when(jnp.logical_not(edge))
    def _():
        pl.semaphore_wait(barrier, 5)

    def block(col, p, direction, oo, ee):
        rows = pl.ds(pl.multiple_of(p * TOK, TOK), TOK)
        big = pltpu.make_async_remote_copy(
            src_ref=x_all.at[col, rows], dst_ref=x_all.at[col, rows],
            send_sem=bx_s.at[direction, p], recv_sem=bx_r.at[col, p],
            device_id=(d, oo, ee), device_id_type=MESH)
        small = pltpu.make_async_remote_copy(
            src_ref=r_all.at[col, p], dst_ref=r_all.at[col, p],
            send_sem=br_s.at[direction, p], recv_sem=br_r.at[col, p],
            device_id=(d, oo, ee), device_id_type=MESH)
        return small, big

    def send(col, p, direction, oo, ee):
        for cp in block(col, p, direction, oo, ee):
            cp.start()

    def arrive(col, p):
        for cp in block(col, p, 0, o, mate):
            cp.wait_recv()

    def sent(col, p, direction):
        for cp in block(col, p, direction, o, mate):
            cp.wait_send()

    xcp.wait()

    @pl.when(o < PLANES - 1)
    def _():
        send(e, o, 0, o + 1, e)

    @pl.when(o > 0)
    def _():
        send(e, o, 1, o - 1, e)

    send(e, o, 2, o, yp)
    send(e, o, 3, o, mate)

    def from_y(p):
        arrive(yp, p)
        send(yp, p, 4, o, mate)

    for dist in range(1, PLANES):
        @pl.when(o >= dist)
        def _():
            p = o - dist
            arrive(e, p)

            @pl.when(o < PLANES - 1)
            def _():
                send(e, p, 0, o + 1, e)

            send(e, p, 2, o, yp)
            send(e, p, 3, o, mate)

        @pl.when(o + dist < PLANES)
        def _():
            p = o + dist
            arrive(e, p)

            @pl.when(o > 0)
            def _():
                send(e, p, 1, o - 1, e)

            send(e, p, 2, o, yp)
            send(e, p, 3, o, mate)

        back = dist - 1

        @pl.when(o >= back)
        def _():
            from_y(o - back)

        if back:
            @pl.when(o + back < PLANES)
            def _():
                from_y(o + back)

    col_i, row_i = iota((CT, CT), 1), iota((CT, CT), 0)
    same = col_i // TOK == row_i // TOK
    before = (same & (row_i < col_i)).astype(BF16)
    after = (same & (col_i < row_i)).astype(BF16)
    eye = (col_i == row_i).astype(BF16)

    def lanes(col):
        r = r_all[col]
        low = iota((TOPK, 128), 1) < TOK
        return jnp.concatenate(
            [jnp.where(low, r[0], r[1]), jnp.where(low, r[2], r[3])], axis=1)

    r_own = lanes(e)
    exp_id = iota((NEXP, CT), 0).astype(F32)
    hot = jnp.zeros((NEXP, CT), F32)
    for k in range(TOPK):
        hot = hot + (r_own[k:k + 1, :] == exp_id).astype(F32)
    hot = hot.astype(BF16)
    chosen = dot_nt(eye, hot)
    pos = dot_nt(after, hot)
    logits = dot(x_all[e], wr_ref[...])
    top = jnp.max(jnp.where(chosen > 0.5, logits, -jnp.inf), axis=1, keepdims=True)
    ex = jnp.where(chosen > 0.5, jnp.exp(logits - top), 0.0)
    gate = ex / jnp.sum(ex, axis=1, keepdims=True)
    pos = jnp.where(chosen > 0.5, pos, -1.0)
    g1 = gate.astype(BF16)
    rest = gate - g1.astype(F32)
    g2 = rest.astype(BF16)
    g3 = (rest - g2.astype(F32)).astype(BF16)
    for q in range(COLS):
        n_i, k_i = iota((NEXP, ROWS), 1), iota((NEXP, ROWS), 0)
        first = (o * COLS + rel[q]) * JLOC
        expand = (k_i == first + n_i // SL).astype(BF16)
        slot = iota((CT, ROWS), 1) % SL
        hit = ((slot // CAP == iota((CT, ROWS), 0) // TOK)
               & (dot(pos.astype(BF16), expand) == (slot % CAP).astype(F32)))
        for k, g in enumerate((g1, g2, g3)):
            wst[q, k * CT:(k + 1) * CT, :] = jnp.where(hit, dot(g, expand), 0.0).astype(BF16)

    mine = ((o * COLS + e) * JLOC).astype(F32)

    def select(col):
        r = lanes(col)
        rows = []
        for j in range(JLOC):
            rows.append(jnp.max((r == mine + j).astype(F32), axis=0, keepdims=True))
        m = jnp.concatenate(rows + [jnp.zeros((8 - JLOC, CT), F32)], axis=0)
        pm = jnp.where(m > 0.5, dot(m.astype(BF16), before), -1.0)
        s_i = iota((SL, CT), 0)
        ok = s_i // CAP == iota((SL, CT), 1) // TOK
        want = (s_i % CAP).astype(F32)
        pieces = [(ok & (pm[j:j + 1, :] == want)).astype(F32) for j in range(JLOC)]
        return jnp.concatenate(pieces, axis=0).astype(BF16)

    def pick(ca, cb, base):
        sa, sb = select(ca), select(cb)
        for n in range(DIM // 512):
            cols = pl.ds(n * 512, 512)
            ra = dot(sa, x_all[ca, :, cols])
            rb = dot(sb, x_all[cb, :, cols])
            for j in range(JLOC):
                both = jnp.concatenate([ra[j * SL:(j + 1) * SL], rb[j * SL:(j + 1) * SL]], axis=0)
                xs[j, base:base + 2 * SL, cols] = both.astype(BF16)

    for p in range(PLANES):
        arrive(mate, p)
    pick(e, mate, 0)

    @pl.when(o == 0)
    def _():
        from_y(o + 3)

    @pl.when(o == PLANES - 1)
    def _():
        from_y(o - 3)

    for p in range(PLANES):
        arrive(diag, p)
    pick(yp, diag, 2 * SL)

    for j in range(JLOC):
        wcp[j][0].wait()
        wcp[j][1].wait()
        for n in range(FF // 512):
            cols = slice(n * 512, (n + 1) * 512)
            ga = dot(xs[j], wgb[j, :, cols])
            up = dot(xs[j], wub[j, :, cols])
            hid[j, :, cols] = (jax.nn.silu(ga) * up).astype(BF16)

    def ycopy(k, q):
        return pltpu.make_async_remote_copy(
            src_ref=ysend.at[k, q - 1], dst_ref=yrecv.at[k, q],
            send_sem=ys_s.at[k, q - 1], recv_sem=ys_r.at[k, q - 1],
            device_id=(d, o, rel[q]), device_id_type=MESH)

    for k in range(NC):
        wd_copy(k).wait()
        outs = [dot(hid[j], wdb[k % 2, j]) for j in range(JLOC)]
        for q in (2, 3, 1, 0):
            rows = jnp.concatenate([r[q * SL:(q + 1) * SL] for r in outs], axis=0).astype(BF16)
            if q:
                ysend[k, q - 1] = rows
                ycopy(k, q).start()
            else:
                yrecv[k, 0] = rows
        if k + 2 < NC:
            wd_copy(k + 2).start()

    def zcopy(k, p, slot, oo):
        return pltpu.make_async_remote_copy(
            src_ref=part.at[k, p], dst_ref=zr.at[k, slot],
            send_sem=zs_s.at[k, p], recv_sem=zs_r.at[k, slot],
            device_id=(d, oo, e), device_id_type=MESH)

    def up(k, p):
        zcopy(k, p, p, o + 1).start()

    def down(k, p):
        @pl.when(o == p + 1)
        def _():
            zcopy(k, p, PLANES, o - 1).start()

        @pl.when(o > p + 1)
        def _():
            zcopy(k, p, p, o - 1).start()

    def sums(k):
        for q in range(1, COLS):
            ycopy(k, q).wait_recv()
        acc = dot(wst[0], yrecv[k, 0])
        for q in range(1, COLS):
            acc = acc + dot(wst[q], yrecv[k, q])
        tot = acc[0:CT] + acc[CT:2 * CT] + acc[2 * CT:3 * CT]
        for p in range(PLANES):
            part[k, p] = tot[p * TOK:(p + 1) * TOK]

        @pl.when(o == 0)
        def _():
            for p in (3, 2, 1):
                up(k, p)

        @pl.when(o == PLANES - 1)
        def _():
            for p in (0, 1, 2):
                down(k, p)

    def relay(k):
        for p in (3, 2):
            @pl.when((o > 0) & (o < p))
            def _():
                zcopy(k, p, p, o).wait_recv()
                part[k, p] = part[k, p] + zr[k, p]
                up(k, p)
        for p in (0, 1):
            @pl.when((o < PLANES - 1) & (o > p))
            def _():
                zcopy(k, p, p, o).wait_recv()
                part[k, p] = part[k, p] + zr[k, p]
                down(k, p)

    def finish(k):
        cols = pl.ds(k * CW, CW)

        @pl.when(o == 0)
        def _():
            zcopy(k, 0, PLANES, o).wait_recv()
            out_ref[:, cols] = (part[k, 0] + zr[k, PLANES]).astype(BF16)

        @pl.when(o == PLANES - 1)
        def _():
            zcopy(k, 0, PLANES - 1, o).wait_recv()
            out_ref[:, cols] = (part[k, PLANES - 1] + zr[k, PLANES - 1]).astype(BF16)

        @pl.when((o > 0) & (o < PLANES - 1))
        def _():
            zcopy(k, 0, o, o).wait_recv()
            zcopy(k, 0, PLANES, o).wait_recv()
            out_ref[:, cols] = (part[k, o] + zr[k, o] + zr[k, PLANES]).astype(BF16)

    sums(0)
    for k in range(1, NC):
        sums(k)
        relay(k - 1)
    relay(NC - 1)
    for k in range(NC):
        finish(k)

    for p in range(PLANES):
        @pl.when((o < PLANES - 1) & (p <= o))
        def _():
            sent(e, p, 0)

        @pl.when((o > 0) & (p >= o))
        def _():
            sent(e, p, 1)

        sent(e, p, 2)
        sent(e, p, 3)
        sent(yp, p, 4)
    for k in range(NC):
        for q in range(1, COLS):
            ycopy(k, q).wait_send()
        for p in range(PLANES):
            @pl.when(o != p)
            def _():
                zcopy(k, p, p, o).wait_send()


def solution(mesh):
    row_spec = P(('data', 'outer', 'expert'), None)
    weight_spec = P(('outer', 'expert'), None, None)
    vmem = pl.BlockSpec(memory_space=pltpu.VMEM)
    anyspace = pl.BlockSpec(memory_space=pl.ANY)
    dma = pltpu.SemaphoreType.DMA

    def per_device(tokens, w_router, routes, w_gate, w_up, w_down):
        return pl.pallas_call(
            kernel,
            name='moe',
            out_shape=jax.ShapeDtypeStruct((TOK, DIM), BF16),
            in_specs=[anyspace, vmem, vmem, anyspace, anyspace, anyspace],
            out_specs=vmem,
            scratch_shapes=[
                pltpu.VMEM((COLS, CT, DIM), BF16),
                pltpu.VMEM((COLS, PLANES, TOPK, 128), F32),
                pltpu.VMEM((JLOC, ROWS, DIM), BF16),
                pltpu.VMEM((JLOC, DIM, FF), BF16),
                pltpu.VMEM((JLOC, DIM, FF), BF16),
                pltpu.VMEM((2, JLOC, FF, CW), BF16),
                pltpu.VMEM((JLOC, ROWS, FF), BF16),
                pltpu.VMEM((NC, COLS - 1, ROWS, CW), BF16),
                pltpu.VMEM((NC, COLS, ROWS, CW), BF16),
                pltpu.VMEM((COLS, 3 * CT, ROWS), BF16),
                pltpu.VMEM((NC, PLANES, TOK, CW), F32),
                pltpu.VMEM((NC, PLANES + 1, TOK, CW), F32),
                dma, dma((2, JLOC)), dma((2,)),
                dma((5, PLANES)), dma((5, PLANES)),
                dma((COLS, PLANES)), dma((COLS, PLANES)),
                dma((NC, COLS - 1)), dma((NC, COLS - 1)),
                dma((NC, PLANES)), dma((NC, PLANES + 1)),
            ],
            compiler_params=pltpu.CompilerParams(
                collective_id=0, has_side_effects=True, vmem_limit_bytes=67043328),
        )(tokens, w_router, routes, w_gate, w_up, w_down)

    return jax.shard_map(
        per_device, mesh=mesh,
        in_specs=(row_spec, P(), row_spec, weight_spec, weight_spec, weight_spec),
        out_specs=row_spec, check_vma=False)
```

time: 265 us -> 114 us (0.43)
  blocking collectives: 134 us -> 0 us
  Pallas kernels: 0 us -> 109 us
  waiting for transfers between devices: 54.2 us -> 0 us
  local copies, waits for them, and re-layouts: 39.6 us -> 5 us
  matrix products: 23.7 us -> 0 us
  other arithmetic: 8.89 us -> 0 us
  starting transfers between devices: 3.78 us -> 0 us
    all_to_all x3 -> x0, blocking collectives: 134 us -> none  [the longest x1 65.9 us: per_device(): recv_buf = lax.all_to_all(send_buf, 'outer', 1, 1, tiled=True)]
    pallas_call x0 -> x1, Pallas kernels: none -> 109 us  [per_device(): pl.pallas_call(kernel, name='moe', out_shape=jax.ShapeDtypeStruct((TOK, D...]
    all_to_all x1 -> x0, waiting for transfers between devices: 54.2 us -> none  [per_device(): back_buf = lax.all_to_all(back_buf, 'outer', 1, 1, tiled=True)]
    dot_general x3 -> x0, matrix products: 23.7 us -> none  [the longest x1 16.6 us: expert_ffn(): jnp.einsum('erf,efd->erd', hidden, w_down, preferred_element_type=jnp.flo...]
    gather x8 -> x0, local copies, waits for them, and re-layouts: 13.6 us -> none  [the longest x2 6.2 us: per_device(): send_buf = jnp.take(tokens, slot_tok, axis=0, mode='fill', fill_value=0)]
    all_to_all x4 -> x0, local copies, waits for them, and re-layouts: 10.3 us -> none  [the longest x1 3.52 us: per_device(): back_buf = lax.all_to_all(back_buf, 'outer', 1, 1, tiled=True)]
    reshape x3 -> x0, local copies, waits for them, and re-layouts: 5.43 us -> none  [the longest x1 4.08 us: per_device(): back_buf.reshape(num_exp * capacity, model_dim)]
    reduce_sum x3 -> x0, other arithmetic: 4.82 us -> none  [the longest x1 4.67 us: per_device(): return jnp.sum(weighted, axis=1).astype(jnp.bfloat16)]
  transfers between devices with their start and end apart: 1 -> 0, of which waited for: 1 -> 0; matrix products, arithmetic and copies ran while one was open for 2% -> 0% of each run, Pallas kernels for 0% -> 0%
where the time goes in v1:
time: 114 us
  Pallas kernels  109 us (96%)
  local copies, waits for them, and re-layouts  5 us (4%)
    pallas_call x1, Pallas kernels, per_device(): pl.pallas_call(kernel, name='moe', out_shape=jax.ShapeDtypeStruct((TOK, D...  109 us
    unnamed x3, local copies, waits for them, and re-layouts  5 us

profile of v1, /device:TPU:0, one launch (start us, length us, event | category | flops | bytes accessed | tf_op | source)
XLA Modules:
  0.0 114.1 jit_solution(15863292797189551632)
XLA Ops:
  0.0 1.4 %copy.8.rt_ref = s32[64,8]{1,0:T(8,128)} copy(s32[64,8]{0,1:T(8,128)} %param.8) | data formatting | bytes 4096 | tf_op args[2]
  1.4 1.9 %copy.7.wr_ref = bf16[2048,64]{1,0:T(8,128)(2,1)} copy(bf16[2048,64]{0,1:T(8,128)(2,1)} %param.7) | data formatting | bytes 524288 | tf_op args[1]
  3.3 109.1 %moe.1 = bf16[64,2048]{1,0:T(8,128)(2,1)} custom-call(bf16[64,2048]{1,0:T(8,128)(2,1)} %x_hbm.1, bf16[2048,64]{1,0:T(8,128)(2,1)} %copy.7.wr_ref, s32[64,8]{1,0:T(8,128)} %copy.8.rt_ref, bf16[4,2048,1024]{2,1,0:T(8,128)(2,1)} %wg_hbm.1, bf16[4,2048,1024]{2,1,0:T(8,128)(2,1)} %wu_hbm.1, bf16[4,1024,2048]{2,1,0:T(8,128)(2,1)} %wd_hbm.1), custom_call_target="tpu_custom_call" | custom-call | tf_op jit(solution)/shard_map/moe/pallas_call | solution.py:397
  112.5 1.7 %copy.10 = bf16[64,2048]{1,0:T(8,128)(2,1)} copy(bf16[64,2048]{1,0:T(8,128)(2,1)} %moe.1) | data formatting | bytes 524288

commit v2 on v1

v2 whole, which is shorter than its diff:
```python
import functools

import jax
import jax.numpy as jnp
from jax import lax
from jax.experimental import pallas as pl
from jax.experimental.pallas import tpu as pltpu
from jax.sharding import PartitionSpec as P

MESH = pl.DeviceIdType.MESH
F32, BF16 = jnp.float32, jnp.bfloat16
PLANES = 4
COLS = 4
JLOC = 4
TOK = 64
TOPK = 8
CAP = 10
DIM = 2048
FF = 1024
NEXP = 64
CW = 256
NC = DIM // CW
SL = PLANES * CAP
ROWS = COLS * SL
CT = PLANES * TOK
HALF = TOK // 2
WSLOT = 4


def iota(shape, dim):
    return lax.broadcasted_iota(jnp.int32, shape, dim)


def dot(a, b):
    return jnp.dot(a, b, preferred_element_type=F32)


def dot_nt(a, b):
    return lax.dot_general(a, b, (((1,), (1,)), ((), ())), preferred_element_type=F32)


def dot_tn(a, b):
    return lax.dot_general(a, b, (((0,), (0,)), ((), ())), preferred_element_type=F32)


def kernel(x_hbm, wr_hbm, rt_ref, wg_hbm, wu_hbm, wd_hbm, out_hbm,
           x_all, r_all, wr, xs, wgb, wub, wdb, hid, ysend, yrecv, wst, part, zr, obuf,
           lsem, wsem, dsem, osem, bx_s, br_s, bx_r, br_r, ys_s, ys_r, zs_s, zs_r):
    d = lax.axis_index('data')
    o = lax.axis_index('outer')
    e = lax.axis_index('expert')
    c = e % 2
    y = e // 2
    mate = e + 1 - 2 * c
    yp = e + 2 - 4 * y
    diag = mate + yp - e
    rel = (e, mate, yp, diag)
    last = PLANES - 1

    own = pl.ds(pl.multiple_of(o * TOK, TOK), TOK)
    xcp = pltpu.make_async_copy(x_hbm, x_all.at[e, own], lsem.at[0])
    xcp.start()

    dup = (iota((TOK, 128), 1) % TOK == iota((TOK, 128), 0)).astype(BF16)
    r_all[e, o] = dot(rt_ref[...].astype(F32).astype(BF16), dup)

    barrier = pltpu.get_barrier_semaphore()

    def greet(oo, ee):
        pl.semaphore_signal(barrier, inc=1, device_id=(d, oo, ee), device_id_type=MESH)

    for q in range(1, 4):
        greet(o, rel[q])

    @pl.when(o > 0)
    def _():
        greet(o - 1, e)

    @pl.when(o < last)
    def _():
        greet(o + 1, e)

    xcp.wait()
    wrcp = pltpu.make_async_copy(wr_hbm, wr, lsem.at[1])
    wrcp.start()
    wcp = []
    for j in range(JLOC):
        a = pltpu.make_async_copy(wg_hbm.at[j], wgb.at[j], wsem.at[0, j])
        b = pltpu.make_async_copy(wu_hbm.at[j], wub.at[j], wsem.at[1, j])
        a.start()
        b.start()
        wcp.append((a, b))

    def wd_copy(k):
        return pltpu.make_async_copy(
            wd_hbm.at[:, :, pl.ds(k * CW, CW)], wdb.at[k % WSLOT], dsem.at[k % WSLOT])

    for k in range(WSLOT):
        wd_copy(k).start()

    edge = (o == 0) | (o == last)

    @pl.when(edge)
    def _():
        pl.semaphore_wait(barrier, 4)

    @pl.when(jnp.logical_not(edge))
    def _():
        pl.semaphore_wait(barrier, 5)

    UP, DOWN, SIDE, MATE, PASS, YUP, YDOWN = range(7)

    def block(col, p, h, direction, oo, ee):
        rows = pl.ds(pl.multiple_of(p * TOK + h * HALF, HALF), HALF)
        cps = [pltpu.make_async_remote_copy(
            src_ref=x_all.at[col, rows], dst_ref=x_all.at[col, rows],
            send_sem=bx_s.at[direction, p, h], recv_sem=bx_r.at[col, p, h],
            device_id=(d, oo, ee), device_id_type=MESH)]
        if h == 0:
            cps.insert(0, pltpu.make_async_remote_copy(
                src_ref=r_all.at[col, p], dst_ref=r_all.at[col, p],
                send_sem=br_s.at[direction, p], recv_sem=br_r.at[col, p],
                device_id=(d, oo, ee), device_id_type=MESH))
        return cps

    def send(col, p, h, direction, oo, ee):
        for cp in block(col, p, h, direction, oo, ee):
            cp.start()

    def arrive(col, p, h):
        for cp in block(col, p, h, 0, o, mate):
            cp.wait_recv()

    def sent(col, p, h, direction):
        for cp in block(col, p, h, direction, o, mate):
            cp.wait_send()

    def sides(dist, fn):
        @pl.when(o >= dist)
        def _():
            fn(o - dist, -1)

        @pl.when(o + dist < PLANES)
        def _():
            fn(o + dist, 1)

    def zget(dist, h):
        def one(p, side):
            arrive(e, p, h)
            if side < 0:
                @pl.when(o < last)
                def _():
                    send(e, p, h, UP, o + 1, e)
            else:
                @pl.when(o > 0)
                def _():
                    send(e, p, h, DOWN, o - 1, e)
            if (dist, h) != (1, 0):
                send(e, p, h, SIDE, o, yp)
            send(e, p, h, MATE, o, mate)

        sides(dist, one)

    def yget(dist, h):
        def one(p, side):
            arrive(yp, p, h)
            send(yp, p, h, PASS, o, mate)

        sides(dist, one)

    for h in range(2):
        @pl.when(o < last)
        def _():
            send(e, o, h, UP, o + 1, e)

        @pl.when(o > 0)
        def _():
            send(e, o, h, DOWN, o - 1, e)

        send(e, o, h, SIDE, o, yp)
        send(e, o, h, MATE, o, mate)

    zget(1, 0)
    arrive(yp, o, 0)

    @pl.when(o < last)
    def _():
        send(yp, o, 0, YUP, o + 1, e)

    @pl.when(o > 0)
    def _():
        send(yp, o, 0, YDOWN, o - 1, e)

    send(yp, o, 0, PASS, o, mate)
    zget(1, 1)
    arrive(yp, o, 1)
    send(yp, o, 1, PASS, o, mate)
    zget(2, 0)
    yget(1, 0)
    zget(2, 1)
    yget(1, 1)
    zget(3, 0)
    yget(2, 0)
    zget(3, 1)
    yget(2, 1)

    col_i, row_i = iota((CT, CT), 1), iota((CT, CT), 0)
    same = col_i // TOK == row_i // TOK
    before = (same & (row_i < col_i)).astype(BF16)
    after = (same & (col_i < row_i)).astype(BF16)
    eye = (col_i == row_i).astype(BF16)

    def lanes(col):
        r = r_all[col]
        low = iota((TOPK, 128), 1) < TOK
        return jnp.concatenate(
            [jnp.where(low, r[0], r[1]), jnp.where(low, r[2], r[3])], axis=1)

    r_own = lanes(e)
    exp_id = iota((NEXP, CT), 0).astype(F32)
    hot = jnp.zeros((NEXP, CT), F32)
    for k in range(TOPK):
        hot = hot + (r_own[k:k + 1, :] == exp_id).astype(F32)
    hot = hot.astype(BF16)
    chosen = dot_nt(eye, hot)
    pos = dot_nt(after, hot)
    wrcp.wait()
    logits = dot_nt(x_all[e], wr[...])
    top = jnp.max(jnp.where(chosen > 0.5, logits, -jnp.inf), axis=1, keepdims=True)
    ex = jnp.where(chosen > 0.5, jnp.exp(logits - top), 0.0)
    gate = ex / jnp.sum(ex, axis=1, keepdims=True)
    pos = jnp.where(chosen > 0.5, pos, -1.0)
    g1 = gate.astype(BF16)
    rest = gate - g1.astype(F32)
    g2 = rest.astype(BF16)
    g3 = (rest - g2.astype(F32)).astype(BF16)
    for q in range(COLS):
        n_i, k_i = iota((NEXP, ROWS), 1), iota((NEXP, ROWS), 0)
        first = (o * COLS + rel[q]) * JLOC
        expand = (k_i == first + n_i // SL).astype(BF16)
        slot = iota((CT, ROWS), 1) % SL
        hit = ((slot // CAP == iota((CT, ROWS), 0) // TOK)
               & (dot(pos.astype(BF16), expand) == (slot % CAP).astype(F32)))
        for k, g in enumerate((g1, g2, g3)):
            wst[q, k * CT:(k + 1) * CT, :] = jnp.where(hit, dot(g, expand), 0.0).astype(BF16)

    mine = ((o * COLS + e) * JLOC).astype(F32)

    def select(col):
        r = lanes(col)
        rows = []
        for j in range(JLOC):
            rows.append(jnp.max((r == mine + j).astype(F32), axis=0, keepdims=True))
        m = jnp.concatenate(rows + [jnp.zeros((8 - JLOC, CT), F32)], axis=0)
        pm = jnp.where(m > 0.5, dot(m.astype(BF16), before), -1.0)
        s_i = iota((SL, CT), 0)
        ok = s_i // CAP == iota((SL, CT), 1) // TOK
        want = (s_i % CAP).astype(F32)
        pieces = [(ok & (pm[j:j + 1, :] == want)).astype(F32) for j in range(JLOC)]
        return jnp.concatenate(pieces, axis=0).astype(BF16)

    def pick(ca, cb, base):
        sa, sb = select(ca), select(cb)
        for n in range(DIM // 512):
            cols = pl.ds(n * 512, 512)
            ra = dot(sa, x_all[ca, :, cols])
            rb = dot(sb, x_all[cb, :, cols])
            for j in range(JLOC):
                both = jnp.concatenate([ra[j * SL:(j + 1) * SL], rb[j * SL:(j + 1) * SL]], axis=0)
                xs[j, base:base + 2 * SL, cols] = both.astype(BF16)

    for p in range(PLANES):
        for h in range(2):
            arrive(mate, p, h)
    pick(e, mate, 0)
    yget(3, 0)
    yget(3, 1)
    for p in range(PLANES):
        for h in range(2):
            arrive(diag, p, h)
    pick(yp, diag, 2 * SL)

    for j in range(JLOC):
        wcp[j][0].wait()
        wcp[j][1].wait()
        for n in range(FF // 512):
            cols = slice(n * 512, (n + 1) * 512)
            ga = dot(xs[j], wgb[j, :, cols])
            up = dot(xs[j], wub[j, :, cols])
            hid[j, :, cols] = (jax.nn.silu(ga) * up).astype(BF16)

    def ycopy(k, q):
        return pltpu.make_async_remote_copy(
            src_ref=ysend.at[k, q - 1], dst_ref=yrecv.at[k, q],
            send_sem=ys_s.at[k, q - 1], recv_sem=ys_r.at[k, q - 1],
            device_id=(d, o, rel[q]), device_id_type=MESH)

    for k in range(NC):
        wd_copy(k).wait()
        outs = [dot(hid[j], wdb[k % WSLOT, j]) for j in range(JLOC)]
        for q in (2, 3, 1, 0):
            rows = jnp.concatenate([r[q * SL:(q + 1) * SL] for r in outs], axis=0).astype(BF16)
            if q:
                ysend[k, q - 1] = rows
                ycopy(k, q).start()
            else:
                yrecv[k, 0] = rows
        if k + WSLOT < NC:
            wd_copy(k + WSLOT).start()

    def zcopy(k, p, slot, oo):
        return pltpu.make_async_remote_copy(
            src_ref=part.at[k, p], dst_ref=zr.at[k, slot],
            send_sem=zs_s.at[k, p], recv_sem=zs_r.at[k, slot],
            device_id=(d, oo, e), device_id_type=MESH)

    def up(k, p):
        zcopy(k, p, p, o + 1).start()

    def down(k, p):
        @pl.when(o == p + 1)
        def _():
            zcopy(k, p, PLANES, o - 1).start()

        @pl.when(o > p + 1)
        def _():
            zcopy(k, p, p, o - 1).start()

    def sums(k):
        for q in range(1, COLS):
            ycopy(k, q).wait_recv()
        acc = dot(wst[0], yrecv[k, 0])
        for q in range(1, COLS):
            acc = acc + dot(wst[q], yrecv[k, q])
        tot = acc[0:CT] + acc[CT:2 * CT] + acc[2 * CT:3 * CT]
        for p in range(PLANES):
            part[k, p] = tot[p * TOK:(p + 1) * TOK]

        @pl.when(o == 0)
        def _():
            for p in (3, 2, 1):
                up(k, p)

        @pl.when(o == PLANES - 1)
        def _():
            for p in (0, 1, 2):
                down(k, p)

    def pass_up(k, p):
        zcopy(k, p, p, o + 1).wait_recv()
        part[k, p] = part[k, p] + zr[k, p]
        up(k, p)

    def pass_down(k, p):
        zcopy(k, p, p, o - 1).wait_recv()
        part[k, p] = part[k, p] + zr[k, p]
        down(k, p)

    def relay_near(k):
        @pl.when(o == 1)
        def _():
            pass_up(k, 3)
            pass_up(k, 2)

        @pl.when(o == 2)
        def _():
            pass_down(k, 0)
            pass_down(k, 1)

    def relay_far(k):
        @pl.when(o == 1)
        def _():
            pass_down(k, 0)

        @pl.when(o == 2)
        def _():
            pass_up(k, 3)

    def ocopy(k):
        cols = pl.ds(k * CW, CW)
        return pltpu.make_async_copy(obuf.at[:, cols], out_hbm.at[:, cols], osem.at[k])

    def finish(k):
        cols = pl.ds(k * CW, CW)

        @pl.when(o == 0)
        def _():
            zcopy(k, 0, PLANES, o + 1).wait_recv()
            obuf[:, cols] = (part[k, 0] + zr[k, PLANES]).astype(BF16)

        @pl.when(o == last)
        def _():
            zcopy(k, 0, last, o - 1).wait_recv()
            obuf[:, cols] = (part[k, last] + zr[k, last]).astype(BF16)

        @pl.when((o > 0) & (o < last))
        def _():
            zcopy(k, 0, o, o + 1).wait_recv()
            zcopy(k, 0, PLANES, o + 1).wait_recv()
            obuf[:, cols] = (part[k, o] + zr[k, o] + zr[k, PLANES]).astype(BF16)

        ocopy(k).start()

    for k in range(NC + 2):
        if k < NC:
            sums(k)
        if 0 <= k - 1 < NC:
            relay_near(k - 1)
        if k >= 2:
            relay_far(k - 2)
    for k in range(NC):
        finish(k)
    for k in range(NC):
        ocopy(k).wait()

    for p in range(PLANES):
        for h in range(2):
            @pl.when((o < last) & (o >= p))
            def _():
                sent(e, p, h, UP)

            @pl.when((o > 0) & (o <= p))
            def _():
                sent(e, p, h, DOWN)

            if h:
                sent(e, p, h, SIDE)
            else:
                @pl.when((o != p - 1) & (o != p + 1))
                def _():
                    sent(e, p, h, SIDE)

            sent(e, p, h, MATE)
            sent(yp, p, h, PASS)

    @pl.when(o < last)
    def _():
        sent(yp, o, 0, YUP)

    @pl.when(o > 0)
    def _():
        sent(yp, o, 0, YDOWN)

    for k in range(NC):
        for q in range(1, COLS):
            ycopy(k, q).wait_send()
        for p in range(PLANES):
            @pl.when(o != p)
            def _():
                zcopy(k, p, p, 0).wait_send()


def solution(mesh):
    row_spec = P(('data', 'outer', 'expert'), None)
    weight_spec = P(('outer', 'expert'), None, None)
    vmem = pl.BlockSpec(memory_space=pltpu.VMEM)
    anyspace = pl.BlockSpec(memory_space=pl.ANY)
    dma = pltpu.SemaphoreType.DMA

    def per_device(tokens, w_router, routes, w_gate, w_up, w_down):
        return pl.pallas_call(
            kernel,
            name='moe',
            out_shape=jax.ShapeDtypeStruct((TOK, DIM), BF16),
            in_specs=[anyspace, anyspace, vmem, anyspace, anyspace, anyspace],
            out_specs=anyspace,
            scratch_shapes=[
                pltpu.VMEM((COLS, CT, DIM), BF16),
                pltpu.VMEM((COLS, PLANES, TOPK, 128), F32),
                pltpu.VMEM((NEXP, DIM), BF16),
                pltpu.VMEM((JLOC, ROWS, DIM), BF16),
                pltpu.VMEM((JLOC, DIM, FF), BF16),
                pltpu.VMEM((JLOC, DIM, FF), BF16),
                pltpu.VMEM((WSLOT, JLOC, FF, CW), BF16),
                pltpu.VMEM((JLOC, ROWS, FF), BF16),
                pltpu.VMEM((NC, COLS - 1, ROWS, CW), BF16),
                pltpu.VMEM((NC, COLS, ROWS, CW), BF16),
                pltpu.VMEM((COLS, 3 * CT, ROWS), BF16),
                pltpu.VMEM((NC, PLANES, TOK, CW), F32),
                pltpu.VMEM((NC, PLANES + 1, TOK, CW), F32),
                pltpu.VMEM((TOK, DIM), BF16),
                dma((2,)), dma((2, JLOC)), dma((WSLOT,)), dma((NC,)),
                dma((7, PLANES, 2)), dma((7, PLANES)),
                dma((COLS, PLANES, 2)), dma((COLS, PLANES)),
                dma((NC, COLS - 1)), dma((NC, COLS - 1)),
                dma((NC, PLANES)), dma((NC, PLANES + 1)),
            ],
            compiler_params=pltpu.CompilerParams(
                collective_id=0, has_side_effects=True, vmem_limit_bytes=67043328),
        )(tokens, w_router.T, routes.T, w_gate, w_up, w_down)

    return jax.shard_map(
        per_device, mesh=mesh,
        in_specs=(row_spec, P(), row_spec, weight_spec, weight_spec, weight_spec),
        out_specs=row_spec, check_vma=False)
```

time: 114 us -> 91.1 us (0.80)
  Pallas kernels: 109 us -> 89.2 us
  local copies, waits for them, and re-layouts: 5 us -> 1.67 us
    pallas_call x1, Pallas kernels: 109 us -> 89.2 us  [per_device(): pl.pallas_call(kernel, name='moe', out_shape=jax.ShapeDtypeStruct((TOK, D...]
    unnamed x3 -> x1, local copies, waits for them, and re-layouts: 5 us -> 1.67 us
where the time goes in v2:
time: 91.1 us; the launch traced here: 90.9 us
  Pallas kernels  89.2 us (98%)
  local copies, waits for them, and re-layouts  1.67 us (2%)
    pallas_call x1, Pallas kernels, per_device(): pl.pallas_call(kernel, name='moe', out_shape=jax.ShapeDtypeStruct((TOK, D...  89.2 us

profile of v2, /device:TPU:0, one launch (start us, length us, event | category | flops | bytes accessed | tf_op | source)
XLA Modules:
  0.0 90.9 jit_solution(15825188500923149784)
XLA Ops:
  0.0 89.2 %moe.1 = bf16[64,2048]{1,0:T(8,128)(2,1)} custom-call(bf16[64,2048]{1,0:T(8,128)(2,1)} %x_hbm.1, bf16[64,2048]{1,0:T(8,128)(2,1)} %bitcast.2, s32[8,64]{1,0:T(8,128)} %bitcast.3, bf16[4,2048,1024]{2,1,0:T(8,128)(2,1)} %wg_hbm.1, bf16[4,2048,1024]{2,1,0:T(8,128)(2,1)} %wu_hbm.1, bf16[4,1024,2048]{2,1,0:T(8,128)(2,1)} %wd_hbm.1), custom_call_target="tpu_custom_call" | custom-call | tf_op jit(solution)/shard_map/moe/pallas_call | solution.py:461
  89.2 1.7 %copy.8 = bf16[64,2048]{1,0:T(8,128)(2,1)} copy(bf16[64,2048]{1,0:T(8,128)(2,1)} %moe.1) | data formatting | bytes 524288

commit v3 on v0

v3 whole, which is shorter than its diff:
```python
import jax
import jax.numpy as jnp
from jax import lax
from jax.experimental import pallas as pl
from jax.experimental.pallas import tpu as pltpu
from jax.sharding import PartitionSpec as P

MESH = pl.DeviceIdType.MESH
F32, BF16 = jnp.float32, jnp.bfloat16
PLANES = 4
COLS = 4
JLOC = 4
TOK = 64
TOPK = 8
CAP = 10
DIM = 2048
FF = 1024
NEXP = 64
CW = 256
NC = DIM // CW
HALF = TOK // 2
WSLOT = 6
GR = JLOC * CAP
MR = 2 * COLS * CAP
CT = 2 * TOK
HT = COLS * CT
NB, OWN, FAR, NEAR = range(4)
OUT, CROSS, SIDE, MATE, PASS, YOUT, YCROSS = range(7)


def iota(shape, dim):
    return lax.broadcasted_iota(jnp.int32, shape, dim)


def dot(a, b):
    return jnp.dot(a, b, preferred_element_type=F32)


def dot_nt(a, b):
    return lax.dot_general(a, b, (((1,), (1,)), ((), ())), preferred_element_type=F32)


def kernel(x_hbm, wr_hbm, rt_ref, wg_hbm, wu_hbm, wd_hbm, out_hbm,
           x_all, r_all, wr, xs, wgb, wub, wdb, hid, ysend, yrecv, wst, part, zr, obuf,
           lsem, wsem, dsem, osem, bx_s, br_s, bx_r, br_r, ys_s, ys_r, zs_s, zs_r):
    d = lax.axis_index('data')
    o = lax.axis_index('outer')
    e = lax.axis_index('expert')
    c = e % 2
    y = e // 2
    mate = e + 1 - 2 * c
    yp = e + 2 - 4 * y
    diag = mate + yp - e
    rel = (e, mate, yp, diag)
    side = o // 2
    nbp = o + 1 - 2 * (o % 2)
    other = PLANES - 1 - o
    planes = (nbp, o, 3 - 3 * side, 2 - side)
    halves = (side, 1 - side)
    end = (o == 0) | (o == PLANES - 1)
    inner = jnp.logical_not(end)

    def at_end(fn):
        pl.when(end)(fn)

    def at_inner(fn):
        pl.when(inner)(fn)

    def rows_of(col, g, h, n):
        p = planes[g]
        start = col * CT + (p % 2) * TOK + h * HALF
        return p // 2, pl.ds(pl.multiple_of(start, HALF), n)

    own_half, own_rows = rows_of(e, OWN, 0, TOK)
    xcp = pltpu.make_async_copy(x_hbm, x_all.at[own_half, own_rows], lsem.at[0])
    xcp.start()

    dup = (iota((TOK, 128), 1) % TOK == iota((TOK, 128), 0)).astype(BF16)
    r_all[side, e, o % 2] = dot(rt_ref[...].astype(F32).astype(BF16), dup)

    barrier = pltpu.get_barrier_semaphore()

    def greet(oo, ee):
        pl.semaphore_signal(barrier, inc=1, device_id=(d, oo, ee), device_id_type=MESH)

    for q in range(1, 4):
        greet(o, rel[q])
    greet(nbp, e)

    @at_inner
    def _():
        greet(other, e)

    xcp.wait()
    wrcp = pltpu.make_async_copy(wr_hbm, wr, lsem.at[1])
    wrcp.start()
    wcp = []
    for j in range(JLOC):
        a = pltpu.make_async_copy(wg_hbm.at[j], wgb.at[j], wsem.at[0, j])
        b = pltpu.make_async_copy(wu_hbm.at[j], wub.at[j], wsem.at[1, j])
        a.start()
        b.start()
        wcp.append((a, b))

    def wd_copy(n):
        return pltpu.make_async_copy(
            wd_hbm.at[:, :, pl.ds((n % NC) * CW, CW)], wdb.at[n % WSLOT], dsem.at[n % WSLOT])

    for n in range(WSLOT):
        wd_copy(n).start()

    @at_end
    def _():
        pl.semaphore_wait(barrier, 4)

    @at_inner
    def _():
        pl.semaphore_wait(barrier, 5)

    def block(col, g, h, direction, oo, ee):
        half, rows = rows_of(col, g, h, HALF)
        cps = [pltpu.make_async_remote_copy(
            src_ref=x_all.at[half, rows], dst_ref=x_all.at[half, rows],
            send_sem=bx_s.at[direction, g, h], recv_sem=bx_r.at[col, planes[g], h],
            device_id=(d, oo, ee), device_id_type=MESH)]
        if h == 0:
            tile = r_all.at[half, col, planes[g] % 2]
            cps.insert(0, pltpu.make_async_remote_copy(
                src_ref=tile, dst_ref=tile,
                send_sem=br_s.at[direction, g], recv_sem=br_r.at[col, planes[g]],
                device_id=(d, oo, ee), device_id_type=MESH))
        return cps

    targets = {OUT: (e, nbp, e), CROSS: (e, other, e), SIDE: (e, o, yp), MATE: (e, o, mate),
               PASS: (yp, o, mate), YOUT: (yp, nbp, e), YCROSS: (yp, other, e)}

    def send(g, h, *directions):
        for direction in directions:
            col, oo, ee = targets[direction]
            for cp in block(col, g, h, direction, oo, ee):
                cp.start()

    def arrive(col, g, h):
        for cp in block(col, g, h, MATE, o, mate):
            cp.wait_recv()

    def sent(g, h, *directions):
        for direction in directions:
            for cp in block(targets[direction][0], g, h, direction, o, mate):
                cp.wait_send()

    def get(g, h, *directions):
        arrive(e, g, h)
        send(g, h, *directions, MATE)

    def yget(g, h, *directions):
        arrive(yp, g, h)
        send(g, h, *directions, PASS)

    @at_end
    def _():
        for h in range(2):
            send(OWN, h, OUT, SIDE, MATE)
        for h in range(2):
            get(NB, h, SIDE)
            yget(OWN, h)
        for h in range(2):
            get(NEAR, h, SIDE)
            yget(NB, h)

    @at_inner
    def _():
        for h in range(2):
            send(OWN, h, OUT, CROSS, SIDE, MATE)
        get(NB, 0, CROSS, SIDE)
        get(NEAR, 0, OUT)
        yget(OWN, 0)
        get(NB, 1, CROSS, SIDE)
        send(OWN, 0, YCROSS)
        get(NEAR, 1, OUT, SIDE)
        yget(OWN, 1)
        get(FAR, 0, OUT)
        yget(NB, 0)
        get(FAR, 1, OUT, SIDE)
        send(FAR, 0, SIDE)
        yget(NB, 1)

    def late_blocks(step):
        if step == 0:
            @at_end
            def _():
                get(FAR, 0, SIDE)
                yget(NEAR, 0)

            @at_inner
            def _():
                yget(NEAR, 0)
                yget(NEAR, 1)
        elif step == 1:
            @at_end
            def _():
                get(FAR, 1)
                yget(NEAR, 1)

            @at_inner
            def _():
                yget(FAR, 1, YOUT)
        else:
            @at_end
            def _():
                yget(FAR, 0)
                yget(FAR, 1)

            @at_inner
            def _():
                yget(FAR, 0)

    def from_mate(g):
        for col in (mate, diag):
            for h in range(2):
                arrive(col, g, h)

    col_i, row_i = iota((CT, CT), 1), iota((CT, CT), 0)
    same = col_i // TOK == row_i // TOK
    before = (same & (row_i < col_i)).astype(BF16)
    after = (same & (col_i < row_i)).astype(BF16)
    eye = (col_i == row_i).astype(BF16)
    low = iota((TOPK, CT), 1) < TOK
    mine = ((o * COLS + e) * JLOC).astype(F32)

    def pick(ps):
        half = halves[ps]
        r = r_all[half]
        routes = jnp.concatenate(
            [jnp.where(low, r[k, 0], r[k, 1]) for k in range(COLS)], axis=1)
        m = [jnp.max((routes == mine + j).astype(F32), axis=0, keepdims=True)
             for j in range(JLOC)]
        m = jnp.concatenate(m + [jnp.zeros((8 - JLOC, HT), F32)], axis=0)
        mb = m.astype(BF16)
        pos = jnp.concatenate(
            [dot(mb[:, k * CT:(k + 1) * CT], before) for k in range(COLS)], axis=1)
        pm = jnp.where(m > 0.5, pos, -1.0)
        ri, ci = iota((MR, HT), 0), iota((MR, HT), 1)
        q = (ri % GR) // CAP
        col = jnp.where(q == 0, rel[0], jnp.where(q == 1, rel[1], jnp.where(q == 2, rel[2], rel[3])))
        par = jnp.where(ri < GR, planes[2 * ps] % 2, planes[2 * ps + 1] % 2)
        want = jnp.where((ci // CT == col) & ((ci // TOK) % 2 == par), ri % CAP, -2).astype(F32)
        sel = jnp.concatenate(
            [(pm[j:j + 1, :] == want).astype(F32) for j in range(JLOC)], axis=0).astype(BF16)
        for n in range(DIM // 512):
            cols = pl.ds(n * 512, 512)
            got = dot(sel, x_all[half, :, cols])
            for j in range(JLOC):
                xs[j, :, cols] = got[j * MR:(j + 1) * MR].astype(BF16)

    def gates(ps):
        half = halves[ps]
        r = r_all[half, e]
        routes = jnp.where(low, r[0], r[1])
        exp_id = iota((NEXP, CT), 0).astype(F32)
        hot = jnp.zeros((NEXP, CT), F32)
        for k in range(TOPK):
            hot = hot + (routes[k:k + 1, :] == exp_id).astype(F32)
        hot = hot.astype(BF16)
        chosen = dot_nt(eye, hot) > 0.5
        pos = jnp.where(chosen, dot_nt(after, hot), -1.0)
        logits = dot_nt(x_all[half, pl.ds(pl.multiple_of(e * CT, CT), CT)], wr[...])
        top = jnp.max(jnp.where(chosen, logits, -jnp.inf), axis=1, keepdims=True)
        ex = jnp.where(chosen, jnp.exp(logits - top), 0.0)
        gate = ex / jnp.sum(ex, axis=1, keepdims=True)
        g1 = gate.astype(BF16)
        rest = gate - g1.astype(F32)
        g2 = rest.astype(BF16)
        g3 = (rest - g2.astype(F32)).astype(BF16)
        pos = pos.astype(BF16)
        slot = (iota((CT, GR), 1) % CAP).astype(F32)
        for q in range(COLS):
            first = (o * COLS + rel[q]) * JLOC
            expand = (iota((NEXP, GR), 0) == first + iota((NEXP, GR), 1) // CAP).astype(BF16)
            hit = dot(pos, expand) == slot
            for k, g in enumerate((g1, g2, g3)):
                w = jnp.where(hit, dot(g, expand), 0.0)
                for i in range(2):
                    par = planes[2 * ps + i] % 2
                    wst[2 * ps + i, q, k * TOK:(k + 1) * TOK, :] = jnp.where(
                        par == 0, w[:TOK], w[TOK:]).astype(BF16)

    def gate_up(ps, j):
        if ps == 0:
            wcp[j][0].wait()
            wcp[j][1].wait()
        for n in range(FF // 512):
            cols = slice(n * 512, (n + 1) * 512)
            ga = dot(xs[j], wgb[j, :, cols])
            gu = dot(xs[j], wub[j, :, cols])
            hid[j, :, cols] = (jax.nn.silu(ga) * gu).astype(BF16)

    def ycopy(g, k, q):
        return pltpu.make_async_remote_copy(
            src_ref=ysend.at[g, k, q - 1], dst_ref=yrecv.at[g, k, q],
            send_sem=ys_s.at[g, k, q - 1], recv_sem=ys_r.at[g, k, q - 1],
            device_id=(d, o, rel[q]), device_id_type=MESH)

    def ystart(g, k):
        for q in (2, 3, 1):
            ycopy(g, k, q).start()

    def down_chunk(ps, k):
        n = ps * NC + k
        wd_copy(n).wait()
        outs = [dot(hid[j], wdb[n % WSLOT, j]) for j in range(JLOC)]
        for i in range(2):
            g = 2 * ps + i
            for q in (2, 3, 1, 0):
                at = i * GR + q * CAP
                rows = jnp.concatenate([r[at:at + CAP] for r in outs], axis=0).astype(BF16)
                if q:
                    ysend[g, k, q - 1] = rows
                else:
                    yrecv[g, k, 0] = rows
            if g != OWN:
                ystart(g, k)
        if n + WSLOT < 2 * NC:
            wd_copy(n + WSLOT).start()

    def zcopy(k, g, slot, oo):
        return pltpu.make_async_remote_copy(
            src_ref=part.at[k, g], dst_ref=zr.at[k, slot],
            send_sem=zs_s.at[k, g], recv_sem=zs_r.at[k, slot],
            device_id=(d, oo, e), device_id_type=MESH)

    def sums(g, k):
        for q in range(1, COLS):
            ycopy(g, k, q).wait_recv()
        acc = dot(wst[g, 0], yrecv[g, k, 0])
        for q in range(1, COLS):
            acc = acc + dot(wst[g, q], yrecv[g, k, q])
        part[k, g] = acc[0:TOK] + acc[TOK:2 * TOK] + acc[2 * TOK:3 * TOK]
        if g != OWN:
            @at_end
            def _():
                zcopy(k, g, {NB: 0, FAR: 1, NEAR: 2}[g], nbp).start()

    def relay(k, g, slot_in, slot_out, oo):
        zcopy(k, g, slot_in, nbp).wait_recv()
        part[k, g] = part[k, g] + zr[k, slot_in]
        zcopy(k, g, slot_out, oo).start()

    def relay_near(k):
        @at_inner
        def _():
            relay(k, FAR, 1, 4, other)
            relay(k, NEAR, 2, 3, other)

    def relay_far(k):
        @at_inner
        def _():
            relay(k, NB, 4, 0, nbp)

    def ocopy(k):
        cols = pl.ds(k * CW, CW)
        return pltpu.make_async_copy(obuf.at[:, cols], out_hbm.at[:, cols], osem.at[k])

    def finish(k):
        cols = pl.ds(k * CW, CW)
        zcopy(k, OWN, 0, nbp).wait_recv()

        @at_end
        def _():
            obuf[:, cols] = (part[k, OWN] + zr[k, 0]).astype(BF16)

        @at_inner
        def _():
            zcopy(k, OWN, 3, nbp).wait_recv()
            obuf[:, cols] = (part[k, OWN] + zr[k, 0] + zr[k, 3]).astype(BF16)

        ocopy(k).start()

    from_mate(OWN)
    from_mate(NB)
    pick(0)
    gate_up(0, 0)
    late_blocks(0)
    gate_up(0, 1)
    gate_up(0, 2)
    late_blocks(1)
    gate_up(0, 3)
    for k in range(3):
        down_chunk(0, k)
    late_blocks(2)
    for k in range(3, NC):
        down_chunk(0, k)
    wrcp.wait()
    gates(0)

    from_mate(NEAR)
    from_mate(FAR)
    pick(1)
    for j in range(JLOC):
        gate_up(1, j)
        sums(NB, 2 * j)
        sums(NB, 2 * j + 1)
    for k in range(NC):
        down_chunk(1, k)
    for k in range(NC):
        ystart(OWN, k)
    gates(1)
    for k in range(NC + 2):
        if k < NC:
            sums(FAR, k)
            sums(NEAR, k)
        if 0 <= k - 1 < NC:
            relay_near(k - 1)
        if k >= 2:
            relay_far(k - 2)
        if 4 <= k < NC:
            sums(OWN, 2 * (k - 4))
            sums(OWN, 2 * (k - 4) + 1)
    for k in range(NC):
        finish(k)
    for k in range(NC):
        ocopy(k).wait()

    for g in range(4):
        for h in range(2):
            sent(g, h, MATE, PASS)

    @at_end
    def _():
        for h in range(2):
            sent(OWN, h, OUT, SIDE)
            sent(NB, h, SIDE)
            sent(NEAR, h, SIDE)
        sent(FAR, 0, SIDE)

    @at_inner
    def _():
        for h in range(2):
            sent(OWN, h, OUT, CROSS, SIDE)
            sent(NB, h, CROSS, SIDE)
            sent(NEAR, h, OUT)
            sent(FAR, h, OUT, SIDE)
        sent(NEAR, 1, SIDE)
        sent(OWN, 0, YCROSS)
        sent(FAR, 1, YOUT)

    for k in range(NC):
        for g in range(4):
            for q in range(1, COLS):
                ycopy(g, k, q).wait_send()
            if g != OWN:
                zcopy(k, g, 0, nbp).wait_send()


def solution(mesh):
    row_spec = P(('data', 'outer', 'expert'), None)
    weight_spec = P(('outer', 'expert'), None, None)
    vmem = pl.BlockSpec(memory_space=pltpu.VMEM)
    anyspace = pl.BlockSpec(memory_space=pl.ANY)
    dma = pltpu.SemaphoreType.DMA

    def per_device(tokens, w_router, routes, w_gate, w_up, w_down):
        return pl.pallas_call(
            kernel,
            name='moe',
            out_shape=jax.ShapeDtypeStruct((TOK, DIM), BF16),
            in_specs=[anyspace, anyspace, vmem, anyspace, anyspace, anyspace],
            out_specs=anyspace,
            scratch_shapes=[
                pltpu.VMEM((2, HT, DIM), BF16),
                pltpu.VMEM((2, COLS, 2, TOPK, 128), F32),
                pltpu.VMEM((NEXP, DIM), BF16),
                pltpu.VMEM((JLOC, MR, DIM), BF16),
                pltpu.VMEM((JLOC, DIM, FF), BF16),
                pltpu.VMEM((JLOC, DIM, FF), BF16),
                pltpu.VMEM((WSLOT, JLOC, FF, CW), BF16),
                pltpu.VMEM((JLOC, MR, FF), BF16),
                pltpu.VMEM((4, NC, COLS - 1, GR, CW), BF16),
                pltpu.VMEM((4, NC, COLS, GR, CW), BF16),
                pltpu.VMEM((4, COLS, 3 * TOK, GR), BF16),
                pltpu.VMEM((NC, 4, TOK, CW), F32),
                pltpu.VMEM((NC, 5, TOK, CW), F32),
                pltpu.VMEM((TOK, DIM), BF16),
                dma((2,)), dma((2, JLOC)), dma((WSLOT,)), dma((NC,)),
                dma((7, 4, 2)), dma((7, 4)),
                dma((COLS, PLANES, 2)), dma((COLS, PLANES)),
                dma((4, NC, COLS - 1)), dma((4, NC, COLS - 1)),
                dma((NC, 4)), dma((NC, 5)),
            ],
            compiler_params=pltpu.CompilerParams(
                collective_id=0, has_side_effects=True, vmem_limit_bytes=67043328),
        )(tokens, w_router.T, routes.T, w_gate, w_up, w_down)

    return jax.shard_map(
        per_device, mesh=mesh,
        in_specs=(row_spec, P(), row_spec, weight_spec, weight_spec, weight_spec),
        out_specs=row_spec, check_vma=False)
```

time: 265 us -> 86.1 us (0.32)
  blocking collectives: 134 us -> 0 us
  Pallas kernels: 0 us -> 84.2 us
  waiting for transfers between devices: 54.2 us -> 0 us
  local copies, waits for them, and re-layouts: 39.6 us -> 1.67 us
  matrix products: 23.7 us -> 0 us
  other arithmetic: 8.89 us -> 0 us
  starting transfers between devices: 3.78 us -> 0 us
    all_to_all x3 -> x0, blocking collectives: 134 us -> none  [the longest x1 65.9 us: per_device(): recv_buf = lax.all_to_all(send_buf, 'outer', 1, 1, tiled=True)]
    pallas_call x0 -> x1, Pallas kernels: none -> 84.2 us  [per_device(): pl.pallas_call(kernel, name='moe', out_shape=jax.ShapeDtypeStruct((TOK, D...]
    all_to_all x1 -> x0, waiting for transfers between devices: 54.2 us -> none  [per_device(): back_buf = lax.all_to_all(back_buf, 'outer', 1, 1, tiled=True)]
    dot_general x3 -> x0, matrix products: 23.7 us -> none  [the longest x1 16.6 us: expert_ffn(): jnp.einsum('erf,efd->erd', hidden, w_down, preferred_element_type=jnp.flo...]
    gather x8 -> x0, local copies, waits for them, and re-layouts: 13.6 us -> none  [the longest x2 6.2 us: per_device(): send_buf = jnp.take(tokens, slot_tok, axis=0, mode='fill', fill_value=0)]
    all_to_all x4 -> x0, local copies, waits for them, and re-layouts: 10.3 us -> none  [the longest x1 3.52 us: per_device(): back_buf = lax.all_to_all(back_buf, 'outer', 1, 1, tiled=True)]
    reshape x3 -> x0, local copies, waits for them, and re-layouts: 5.43 us -> none  [the longest x1 4.08 us: per_device(): back_buf.reshape(num_exp * capacity, model_dim)]
    reduce_sum x3 -> x0, other arithmetic: 4.82 us -> none  [the longest x1 4.67 us: per_device(): return jnp.sum(weighted, axis=1).astype(jnp.bfloat16)]
  transfers between devices with their start and end apart: 1 -> 0, of which waited for: 1 -> 0; matrix products, arithmetic and copies ran while one was open for 2% -> 0% of each run, Pallas kernels for 0% -> 0%
where the time goes in v3:
time: 86.1 us; the launch traced here: 85.9 us
  Pallas kernels  84.2 us (98%)
  local copies, waits for them, and re-layouts  1.67 us (2%)
    pallas_call x1, Pallas kernels, per_device(): pl.pallas_call(kernel, name='moe', out_shape=jax.ShapeDtypeStruct((TOK, D...  84.2 us

profile of v3, /device:TPU:0, one launch (start us, length us, event | category | flops | bytes accessed | tf_op | source)
XLA Modules:
  0.0 85.9 jit_solution(5016373508017519556)
XLA Ops:
  0.0 84.2 %moe.1 = bf16[64,2048]{1,0:T(8,128)(2,1)} custom-call(bf16[64,2048]{1,0:T(8,128)(2,1)} %x_hbm.1, bf16[64,2048]{1,0:T(8,128)(2,1)} %bitcast.2, s32[8,64]{1,0:T(8,128)} %bitcast.3, bf16[4,2048,1024]{2,1,0:T(8,128)(2,1)} %wg_hbm.1, bf16[4,2048,1024]{2,1,0:T(8,128)(2,1)} %wu_hbm.1, bf16[4,1024,2048]{2,1,0:T(8,128)(2,1)} %wd_hbm.1), custom_call_target="tpu_custom_call" | custom-call | tf_op jit(solution)/shard_map/moe/pallas_call | solution.py:463
  84.2 1.7 %copy.8 = bf16[64,2048]{1,0:T(8,128)(2,1)} copy(bf16[64,2048]{1,0:T(8,128)(2,1)} %moe.1) | data formatting | bytes 524288

commit v4 on v3

--- a/solution.py
+++ b/solution.py
@@ -22,6 +22,7 @@
 WSLOT = 6
 GR = JLOC * CAP
 MR = 2 * COLS * CAP
+SW = COLS * GR
 CT = 2 * TOK
 HT = COLS * CT
 NB, OWN, FAR, NEAR = range(4)
@@ -164,9 +165,8 @@
         for h in range(2):
             get(NB, h, SIDE)
             yget(OWN, h)
-        for h in range(2):
-            get(NEAR, h, SIDE)
-            yget(NB, h)
+        get(NEAR, 0, SIDE)
+        yget(NB, 0)
 
     @at_inner
     def _():
@@ -181,9 +181,18 @@
         yget(OWN, 1)
         get(FAR, 0, OUT)
         yget(NB, 0)
-        get(FAR, 1, OUT, SIDE)
-        send(FAR, 0, SIDE)
-        yget(NB, 1)
+
+    def mid_blocks():
+        @at_end
+        def _():
+            get(NEAR, 1, SIDE)
+            yget(NB, 1)
+
+        @at_inner
+        def _():
+            get(FAR, 1, OUT, SIDE)
+            send(FAR, 0, SIDE)
+            yget(NB, 1)
 
     def late_blocks(step):
         if step == 0:
@@ -273,17 +282,19 @@
         g2 = rest.astype(BF16)
         g3 = (rest - g2.astype(F32)).astype(BF16)
         pos = pos.astype(BF16)
-        slot = (iota((CT, GR), 1) % CAP).astype(F32)
-        for q in range(COLS):
-            first = (o * COLS + rel[q]) * JLOC
-            expand = (iota((NEXP, GR), 0) == first + iota((NEXP, GR), 1) // CAP).astype(BF16)
-            hit = dot(pos, expand) == slot
-            for k, g in enumerate((g1, g2, g3)):
-                w = jnp.where(hit, dot(g, expand), 0.0)
-                for i in range(2):
-                    par = planes[2 * ps + i] % 2
-                    wst[2 * ps + i, q, k * TOK:(k + 1) * TOK, :] = jnp.where(
-                        par == 0, w[:TOK], w[TOK:]).astype(BF16)
+        slot = (iota((CT, SW), 1) % CAP).astype(F32)
+        n_i = iota((NEXP, SW), 1)
+        q = n_i // GR
+        col = jnp.where(q == 0, rel[0], jnp.where(q == 1, rel[1], jnp.where(q == 2, rel[2], rel[3])))
+        expert = (o * COLS + col) * JLOC + (n_i % GR) // CAP
+        expand = (iota((NEXP, SW), 0) == expert).astype(BF16)
+        hit = dot(pos, expand) == slot
+        for k, g in enumerate((g1, g2, g3)):
+            w = jnp.where(hit, dot(g, expand), 0.0)
+            for i in range(2):
+                par = planes[2 * ps + i] % 2
+                wst[2 * ps + i, k * TOK:(k + 1) * TOK, :] = jnp.where(
+                    par == 0, w[:TOK], w[TOK:]).astype(BF16)
 
     def gate_up(ps, j):
         if ps == 0:
@@ -318,7 +329,7 @@
                     ysend[g, k, q - 1] = rows
                 else:
                     yrecv[g, k, 0] = rows
-            if g != OWN:
+            if g in (NB, FAR):
                 ystart(g, k)
         if n + WSLOT < 2 * NC:
             wd_copy(n + WSLOT).start()
@@ -329,30 +340,35 @@
             send_sem=zs_s.at[k, g], recv_sem=zs_r.at[k, slot],
             device_id=(d, oo, e), device_id_type=MESH)
 
-    def sums(g, k):
-        for q in range(1, COLS):
-            ycopy(g, k, q).wait_recv()
-        acc = dot(wst[g, 0], yrecv[g, k, 0])
-        for q in range(1, COLS):
-            acc = acc + dot(wst[g, q], yrecv[g, k, q])
-        part[k, g] = acc[0:TOK] + acc[TOK:2 * TOK] + acc[2 * TOK:3 * TOK]
+    def sums(g, *chunks):
+        for k in chunks:
+            for q in range(1, COLS):
+                ycopy(g, k, q).wait_recv()
+        for k in chunks:
+            acc = dot(wst[g], yrecv[g, k].reshape(SW, CW))
+            part[k, g] = acc[0:TOK] + acc[TOK:2 * TOK] + acc[2 * TOK:3 * TOK]
         if g != OWN:
             @at_end
             def _():
-                zcopy(k, g, {NB: 0, FAR: 1, NEAR: 2}[g], nbp).start()
+                for k in chunks:
+                    zcopy(k, g, {NB: 0, FAR: 1, NEAR: 2}[g], nbp).start()
 
     def relay(k, g, slot_in, slot_out, oo):
         zcopy(k, g, slot_in, nbp).wait_recv()
         part[k, g] = part[k, g] + zr[k, slot_in]
         zcopy(k, g, slot_out, oo).start()
 
+    def relay_far(k):
+        @at_inner
+        def _():
+            relay(k, FAR, 1, 4, other)
+
     def relay_near(k):
         @at_inner
         def _():
-            relay(k, FAR, 1, 4, other)
             relay(k, NEAR, 2, 3, other)
 
-    def relay_far(k):
+    def relay_back(k):
         @at_inner
         def _():
             relay(k, NB, 4, 0, nbp)
@@ -376,6 +392,9 @@
 
         ocopy(k).start()
 
+    wrcp.wait()
+    gates(0)
+    mid_blocks()
     from_mate(OWN)
     from_mate(NB)
     pick(0)
@@ -385,37 +404,43 @@
     gate_up(0, 2)
     late_blocks(1)
     gate_up(0, 3)
-    for k in range(3):
+    for k in range(NC):
+        if k == NC - 1:
+            late_blocks(2)
         down_chunk(0, k)
-    late_blocks(2)
-    for k in range(3, NC):
-        down_chunk(0, k)
-    wrcp.wait()
-    gates(0)
 
     from_mate(NEAR)
     from_mate(FAR)
     pick(1)
     for j in range(JLOC):
         gate_up(1, j)
-        sums(NB, 2 * j)
-        sums(NB, 2 * j + 1)
+        sums(NB, 2 * j, 2 * j + 1)
+    lead = 4
     for k in range(NC):
         down_chunk(1, k)
+        if k == 3:
+            gates(1)
+        if k >= lead:
+            sums(FAR, k - lead)
+    for k in range(NC):
+        ystart(NEAR, k)
     for k in range(NC):
         ystart(OWN, k)
-    gates(1)
-    for k in range(NC + 2):
-        if k < NC:
-            sums(FAR, k)
-            sums(NEAR, k)
-        if 0 <= k - 1 < NC:
+    for k in range(NC):
+        if k + lead < NC:
+            sums(FAR, k + lead)
+        relay_far(k)
+        if k >= 4:
+            relay_back(k - 4)
+    for k in range(NC):
+        sums(NEAR, k)
+        if k >= 1:
             relay_near(k - 1)
-        if k >= 2:
-            relay_far(k - 2)
-        if 4 <= k < NC:
-            sums(OWN, 2 * (k - 4))
-            sums(OWN, 2 * (k - 4) + 1)
+        if k < 4:
+            relay_back(k + 4)
+        else:
+            sums(OWN, 2 * (k - 4), 2 * (k - 4) + 1)
+    relay_near(NC - 1)
     for k in range(NC):
         finish(k)
     for k in range(NC):
@@ -477,7 +502,7 @@
                 pltpu.VMEM((JLOC, MR, FF), BF16),
                 pltpu.VMEM((4, NC, COLS - 1, GR, CW), BF16),
                 pltpu.VMEM((4, NC, COLS, GR, CW), BF16),
-                pltpu.VMEM((4, COLS, 3 * TOK, GR), BF16),
+                pltpu.VMEM((4, 3 * TOK, SW), BF16),
                 pltpu.VMEM((NC, 4, TOK, CW), F32),
                 pltpu.VMEM((NC, 5, TOK, CW), F32),
                 pltpu.VMEM((TOK, DIM), BF16),

time: 86.1 us -> 78.6 us (0.913)
  the two profiles are of different devices: /device:TPU:0 before, /device:TPU:8 now
where the time goes in v4:
time: 78.6 us; the launch traced here: 78.4 us
  Pallas kernels  76.7 us (98%)
  local copies, waits for them, and re-layouts  1.67 us (2%)
    pallas_call x1, Pallas kernels, per_device(): pl.pallas_call(kernel, name='moe', out_shape=jax.ShapeDtypeStruct((TOK, D...  76.7 us
    unnamed x1, local copies, waits for them, and re-layouts  1.67 us

profile of v4, /device:TPU:8, one launch (start us, length us, event | category | flops | bytes accessed | tf_op | source)
XLA Modules:
  0.0 78.4 jit_solution(11119849718494129561)
XLA Ops:
  0.0 76.7 %moe.1 = bf16[64,2048]{1,0:T(8,128)(2,1)} custom-call(bf16[64,2048]{1,0:T(8,128)(2,1)} %x_hbm.1, bf16[64,2048]{1,0:T(8,128)(2,1)} %bitcast.2, s32[8,64]{1,0:T(8,128)} %bitcast.3, bf16[4,2048,1024]{2,1,0:T(8,128)(2,1)} %wg_hbm.1, bf16[4,2048,1024]{2,1,0:T(8,128)(2,1)} %wu_hbm.1, bf16[4,1024,2048]{2,1,0:T(8,128)(2,1)} %wd_hbm.1), custom_call_target="tpu_custom_call" | custom-call | tf_op jit(solution)/shard_map/moe/pallas_call | solution.py:488
  76.7 1.7 %copy.8 = bf16[64,2048]{1,0:T(8,128)(2,1)} copy(bf16[64,2048]{1,0:T(8,128)(2,1)} %moe.1) | data formatting | bytes 524288

commit v5 on v4

--- a/solution.py
+++ b/solution.py
@@ -18,7 +18,7 @@
 NEXP = 64
 CW = 256
 NC = DIM // CW
-HALF = TOK // 2
+DIRECT = 3
 WSLOT = 6
 GR = JLOC * CAP
 MR = 2 * COLS * CAP
@@ -26,7 +26,7 @@
 CT = 2 * TOK
 HT = COLS * CT
 NB, OWN, FAR, NEAR = range(4)
-OUT, CROSS, SIDE, MATE, PASS, YOUT, YCROSS = range(7)
+OUT, CROSS, SIDE, MATE, PASS, YCROSS = range(6)
 
 
 def iota(shape, dim):
@@ -41,8 +41,8 @@
     return lax.dot_general(a, b, (((1,), (1,)), ((), ())), preferred_element_type=F32)
 
 
-def kernel(x_hbm, wr_hbm, rt_ref, wg_hbm, wu_hbm, wd_hbm, out_hbm,
-           x_all, r_all, wr, xs, wgb, wub, wdb, hid, ysend, yrecv, wst, part, zr, obuf,
+def kernel(x_hbm, wr_hbm, rt_hbm, wg_hbm, wu_hbm, wd_hbm, out_hbm,
+           x_all, r_all, wr, rt, sel, xs, wgb, wub, wdb, hid, ysend, yrecv, wst, part, zr, obuf,
            lsem, wsem, dsem, osem, bx_s, br_s, bx_r, br_r, ys_s, ys_r, zs_s, zs_r):
     d = lax.axis_index('data')
     o = lax.axis_index('outer')
@@ -67,17 +67,16 @@
     def at_inner(fn):
         pl.when(inner)(fn)
 
-    def rows_of(col, g, h, n):
+    def rows_of(col, g, i, n):
         p = planes[g]
-        start = col * CT + (p % 2) * TOK + h * HALF
-        return p // 2, pl.ds(pl.multiple_of(start, HALF), n)
-
-    own_half, own_rows = rows_of(e, OWN, 0, TOK)
+        start = col * CT + (p % 2) * TOK + i * (TOK // n)
+        return p // 2, pl.ds(pl.multiple_of(start, TOK // n), TOK // n)
+
+    own_half, own_rows = rows_of(e, OWN, 0, 1)
     xcp = pltpu.make_async_copy(x_hbm, x_all.at[own_half, own_rows], lsem.at[0])
     xcp.start()
-
-    dup = (iota((TOK, 128), 1) % TOK == iota((TOK, 128), 0)).astype(BF16)
-    r_all[side, e, o % 2] = dot(rt_ref[...].astype(F32).astype(BF16), dup)
+    rtcp = pltpu.make_async_copy(rt_hbm, rt, lsem.at[2])
+    rtcp.start()
 
     barrier = pltpu.get_barrier_semaphore()
 
@@ -88,9 +87,18 @@
         greet(o, rel[q])
     greet(nbp, e)
 
+    @at_end
+    def _():
+        greet(planes[NEAR], e)
+
     @at_inner
     def _():
         greet(other, e)
+        greet(planes[FAR], e)
+
+    rtcp.wait()
+    dup = (iota((TOK, 128), 1) % TOK == iota((TOK, 128), 0)).astype(BF16)
+    r_all[side, e, o % 2] = dot(rt[...].astype(F32).astype(BF16), dup)
 
     xcp.wait()
     wrcp = pltpu.make_async_copy(wr_hbm, wr, lsem.at[1])
@@ -112,19 +120,22 @@
 
     @at_end
     def _():
-        pl.semaphore_wait(barrier, 4)
+        pl.semaphore_wait(barrier, 5)
 
     @at_inner
     def _():
-        pl.semaphore_wait(barrier, 5)
-
-    def block(col, g, h, direction, oo, ee):
-        half, rows = rows_of(col, g, h, HALF)
+        pl.semaphore_wait(barrier, 6)
+
+    def count(g, direction=MATE):
+        return 4 if g == FAR or (g, direction) == (NB, CROSS) else 2
+
+    def block(col, g, i, n, direction, oo, ee):
+        half, rows = rows_of(col, g, i, n)
         cps = [pltpu.make_async_remote_copy(
             src_ref=x_all.at[half, rows], dst_ref=x_all.at[half, rows],
-            send_sem=bx_s.at[direction, g, h], recv_sem=bx_r.at[col, planes[g], h],
+            send_sem=bx_s.at[direction, g, i], recv_sem=bx_r.at[col, planes[g], i],
             device_id=(d, oo, ee), device_id_type=MESH)]
-        if h == 0:
+        if i == 0:
             tile = r_all.at[half, col, planes[g] % 2]
             cps.insert(0, pltpu.make_async_remote_copy(
                 src_ref=tile, dst_ref=tile,
@@ -133,54 +144,68 @@
         return cps
 
     targets = {OUT: (e, nbp, e), CROSS: (e, other, e), SIDE: (e, o, yp), MATE: (e, o, mate),
-               PASS: (yp, o, mate), YOUT: (yp, nbp, e), YCROSS: (yp, other, e)}
-
-    def send(g, h, *directions):
+               PASS: (yp, o, mate), YCROSS: (yp, other, e)}
+
+    def pieces(g, i, direction):
+        n, base = count(g, direction), count(g)
+        return n, range(i * n // base, (i + 1) * n // base)
+
+    def send(g, i, *directions):
         for direction in directions:
             col, oo, ee = targets[direction]
-            for cp in block(col, g, h, direction, oo, ee):
-                cp.start()
-
-    def arrive(col, g, h):
-        for cp in block(col, g, h, MATE, o, mate):
+            n, parts = pieces(g, i, direction)
+            for k in parts:
+                for cp in block(col, g, k, n, direction, oo, ee):
+                    cp.start()
+
+    def arrive(col, g, i):
+        for cp in block(col, g, i, count(g), MATE, o, mate):
             cp.wait_recv()
 
-    def sent(g, h, *directions):
+    def sent(g, i, *directions):
         for direction in directions:
-            for cp in block(targets[direction][0], g, h, direction, o, mate):
-                cp.wait_send()
-
-    def get(g, h, *directions):
-        arrive(e, g, h)
-        send(g, h, *directions, MATE)
-
-    def yget(g, h, *directions):
-        arrive(yp, g, h)
-        send(g, h, *directions, PASS)
-
-    @at_end
-    def _():
-        for h in range(2):
-            send(OWN, h, OUT, SIDE, MATE)
-        for h in range(2):
-            get(NB, h, SIDE)
-            yget(OWN, h)
-        get(NEAR, 0, SIDE)
-        yget(NB, 0)
-
-    @at_inner
-    def _():
-        for h in range(2):
-            send(OWN, h, OUT, CROSS, SIDE, MATE)
-        get(NB, 0, CROSS, SIDE)
-        get(NEAR, 0, OUT)
-        yget(OWN, 0)
-        get(NB, 1, CROSS, SIDE)
-        send(OWN, 0, YCROSS)
-        get(NEAR, 1, OUT, SIDE)
-        yget(OWN, 1)
-        get(FAR, 0, OUT)
-        yget(NB, 0)
+            n, parts = pieces(g, i, direction)
+            for k in parts:
+                for cp in block(targets[direction][0], g, k, n, direction, o, mate):
+                    cp.wait_send()
+
+    def get(g, i, *directions):
+        arrive(e, g, i)
+        send(g, i, *directions, MATE)
+
+    def yget(g, i, *directions):
+        arrive(yp, g, i)
+        send(g, i, *directions, PASS)
+
+    def from_mate(g, i):
+        arrive(mate, g, i)
+        arrive(diag, g, i)
+
+    def early_blocks():
+        @at_end
+        def _():
+            for h in range(2):
+                send(OWN, h, OUT, SIDE, MATE)
+            for h in range(2):
+                get(NB, h, SIDE)
+                yget(OWN, h)
+            get(NEAR, 0, SIDE)
+            yget(NB, 0)
+
+        @at_inner
+        def _():
+            for h in range(2):
+                send(OWN, h, OUT, CROSS, SIDE, MATE)
+            get(NB, 0, CROSS, SIDE)
+            get(NEAR, 0, OUT)
+            yget(OWN, 0)
+            get(NB, 1, CROSS, SIDE)
+            send(OWN, 0, YCROSS)
+            get(NEAR, 1, OUT, SIDE)
+            yget(OWN, 1)
+            get(FAR, 0, OUT, SIDE)
+            get(FAR, 1, OUT, SIDE)
+            yget(NB, 0)
 
     def mid_blocks():
         @at_end
@@ -190,44 +215,27 @@
 
         @at_inner
         def _():
-            get(FAR, 1, OUT, SIDE)
-            send(FAR, 0, SIDE)
+            get(FAR, 2, OUT, SIDE)
+            get(FAR, 3, OUT, SIDE)
             yget(NB, 1)
 
+    zlate = ([(FAR, 0)], [(FAR, 1)], [(FAR, 2)], [(FAR, 3)], [], [], [], [])
+    ylate_end = ([], [(NEAR, 0)], [], [(NEAR, 1)], [(FAR, 0)], [(FAR, 1)], [(FAR, 2)], [(FAR, 3)])
+    ylate_inner = ([(NEAR, 0)], [(NEAR, 1)], [(FAR, 0), (FAR, 1)], [(FAR, 2)], [(FAR, 3)], [], [], [])
+
     def late_blocks(step):
-        if step == 0:
-            @at_end
-            def _():
-                get(FAR, 0, SIDE)
-                yget(NEAR, 0)
-
+        @at_end
+        def _():
+            for g, i in zlate[step]:
+                get(g, i, SIDE)
+            for g, i in ylate_end[step]:
+                yget(g, i)
+
+        if ylate_inner[step]:
             @at_inner
             def _():
-                yget(NEAR, 0)
-                yget(NEAR, 1)
-        elif step == 1:
-            @at_end
-            def _():
-                get(FAR, 1)
-                yget(NEAR, 1)
-
-            @at_inner
-            def _():
-                yget(FAR, 1, YOUT)
-        else:
-            @at_end
-            def _():
-                yget(FAR, 0)
-                yget(FAR, 1)
-
-            @at_inner
-            def _():
-                yget(FAR, 0)
-
-    def from_mate(g):
-        for col in (mate, diag):
-            for h in range(2):
-                arrive(col, g, h)
+                for g, i in ylate_inner[step]:
+                    yget(g, i)
 
     col_i, row_i = iota((CT, CT), 1), iota((CT, CT), 0)
     same = col_i // TOK == row_i // TOK
@@ -237,7 +245,7 @@
     low = iota((TOPK, CT), 1) < TOK
     mine = ((o * COLS + e) * JLOC).astype(F32)
 
-    def pick(ps):
+    def choose(ps):
         half = halves[ps]
         r = r_all[half]
         routes = jnp.concatenate(
@@ -254,11 +262,13 @@
         col = jnp.where(q == 0, rel[0], jnp.where(q == 1, rel[1], jnp.where(q == 2, rel[2], rel[3])))
         par = jnp.where(ri < GR, planes[2 * ps] % 2, planes[2 * ps + 1] % 2)
         want = jnp.where((ci // CT == col) & ((ci // TOK) % 2 == par), ri % CAP, -2).astype(F32)
-        sel = jnp.concatenate(
+        sel[...] = jnp.concatenate(
             [(pm[j:j + 1, :] == want).astype(F32) for j in range(JLOC)], axis=0).astype(BF16)
+
+    def pick(ps):
         for n in range(DIM // 512):
             cols = pl.ds(n * 512, 512)
-            got = dot(sel, x_all[half, :, cols])
+            got = dot(sel[...], x_all[halves[ps], :, cols])
             for j in range(JLOC):
                 xs[j, :, cols] = got[j * MR:(j + 1) * MR].astype(BF16)
 
@@ -329,8 +339,8 @@
                     ysend[g, k, q - 1] = rows
                 else:
                     yrecv[g, k, 0] = rows
-            if g in (NB, FAR):
-                ystart(g, k)
+        if ps == 0:
+            ystart(NB, k)
         if n + WSLOT < 2 * NC:
             wd_copy(n + WSLOT).start()
 
@@ -347,11 +357,9 @@
         for k in chunks:
             acc = dot(wst[g], yrecv[g, k].reshape(SW, CW))
             part[k, g] = acc[0:TOK] + acc[TOK:2 * TOK] + acc[2 * TOK:3 * TOK]
-        if g != OWN:
-            @at_end
-            def _():
-                for k in chunks:
-                    zcopy(k, g, {NB: 0, FAR: 1, NEAR: 2}[g], nbp).start()
+
+    def zsend(k, g, slot, oo):
+        zcopy(k, g, slot, oo).start()
 
     def relay(k, g, slot_in, slot_out, oo):
         zcopy(k, g, slot_in, nbp).wait_recv()
@@ -359,115 +367,165 @@
         zcopy(k, g, slot_out, oo).start()
 
     def relay_far(k):
-        @at_inner
-        def _():
-            relay(k, FAR, 1, 4, other)
+        relay(k, FAR, 1, 4, other)
 
     def relay_near(k):
-        @at_inner
-        def _():
-            relay(k, NEAR, 2, 3, other)
+        relay(k, NEAR, 2, 3, other)
 
     def relay_back(k):
-        @at_inner
-        def _():
-            relay(k, NB, 4, 0, nbp)
+        relay(k, NB, 4, 0, nbp)
 
     def ocopy(k):
         cols = pl.ds(k * CW, CW)
         return pltpu.make_async_copy(obuf.at[:, cols], out_hbm.at[:, cols], osem.at[k])
 
-    def finish(k):
+    def finish(k, *slots):
         cols = pl.ds(k * CW, CW)
-        zcopy(k, OWN, 0, nbp).wait_recv()
-
-        @at_end
-        def _():
-            obuf[:, cols] = (part[k, OWN] + zr[k, 0]).astype(BF16)
-
-        @at_inner
-        def _():
-            zcopy(k, OWN, 3, nbp).wait_recv()
-            obuf[:, cols] = (part[k, OWN] + zr[k, 0] + zr[k, 3]).astype(BF16)
-
+        total = None
+        for slot in slots:
+            zcopy(k, OWN, slot, nbp).wait_recv()
+        total = part[k, OWN]
+        for slot in slots:
+            total = total + zr[k, slot]
+        obuf[:, cols] = total.astype(BF16)
         ocopy(k).start()
 
+    early_blocks()
     wrcp.wait()
     gates(0)
+    from_mate(OWN, 0)
+    from_mate(NB, 0)
+    choose(0)
     mid_blocks()
-    from_mate(OWN)
-    from_mate(NB)
+    from_mate(OWN, 1)
+    from_mate(NB, 1)
     pick(0)
-    gate_up(0, 0)
-    late_blocks(0)
-    gate_up(0, 1)
-    gate_up(0, 2)
-    late_blocks(1)
-    gate_up(0, 3)
+    for j in range(JLOC):
+        gate_up(0, j)
+        late_blocks(j)
     for k in range(NC):
-        if k == NC - 1:
-            late_blocks(2)
         down_chunk(0, k)
-
-    from_mate(NEAR)
-    from_mate(FAR)
+        if k % 2:
+            late_blocks(JLOC + k // 2)
+
+    def sums_nb(*chunks):
+        sums(NB, *chunks)
+
+        @at_end
+        def _():
+            for k in chunks:
+                zsend(k, NB, 0, nbp)
+
+    from_mate(NEAR, 0)
+    from_mate(NEAR, 1)
+    from_mate(FAR, 0)
+    choose(1)
+    sums_nb(0, 1)
+    for i in range(1, 4):
+        from_mate(FAR, i)
     pick(1)
     for j in range(JLOC):
         gate_up(1, j)
-        sums(NB, 2 * j, 2 * j + 1)
+        if j < JLOC - 1:
+            sums_nb(2 * j + 2, 2 * j + 3)
+
+    def sums_far(k):
+        sums(FAR, k)
+        zsend(k, FAR, 1, nbp)
+
     lead = 4
+    relayed = tuple(range(DIRECT, NC))
     for k in range(NC):
         down_chunk(1, k)
-        if k == 3:
+        if k == lead - 1:
             gates(1)
-        if k >= lead:
-            sums(FAR, k - lead)
-    for k in range(NC):
-        ystart(NEAR, k)
-    for k in range(NC):
-        ystart(OWN, k)
-    for k in range(NC):
-        if k + lead < NC:
-            sums(FAR, k + lead)
-        relay_far(k)
-        if k >= 4:
-            relay_back(k - 4)
-    for k in range(NC):
-        sums(NEAR, k)
-        if k >= 1:
-            relay_near(k - 1)
-        if k < 4:
-            relay_back(k + 4)
-        else:
-            sums(OWN, 2 * (k - 4), 2 * (k - 4) + 1)
-    relay_near(NC - 1)
-    for k in range(NC):
-        finish(k)
+
+        @at_end
+        def _():
+            ystart(FAR, k)
+            if k >= lead:
+                sums_far(k - lead)
+
+        @at_inner
+        def _():
+            if k < DIRECT:
+                ystart(NEAR, k)
+            if k == DIRECT - 1:
+                for m in range(DIRECT):
+                    ystart(FAR, m)
+            if k >= DIRECT:
+                ystart(FAR, k)
+            if lead <= k < lead + DIRECT:
+                sums(NEAR, k - lead)
+                zsend(k - lead, NEAR, 3, other)
+
+    @at_end
+    def _():
+        for k in relayed + tuple(range(DIRECT)):
+            ystart(NEAR, k)
+        for k in range(NC):
+            ystart(OWN, k)
+        for k in range(lead, NC):
+            sums_far(k)
+        for k in relayed:
+            sums(NEAR, k)
+            zsend(k, NEAR, 2, nbp)
+        for k in range(DIRECT):
+            sums(NEAR, k)
+            zsend(k, NEAR, 2, planes[NEAR])
+        for k in range(0, NC, 2):
+            sums(OWN, k, k + 1)
+        for k in range(NC):
+            finish(k, 0)
+
+    @at_inner
+    def _():
+        for k in relayed:
+            ystart(NEAR, k)
+        for k in range(NC):
+            ystart(OWN, k)
+        for k in range(NC):
+            sums(FAR, k)
+            relay_far(k)
+            if k >= 4:
+                relay_back(k - 4)
+        for n, k in enumerate(relayed):
+            sums(NEAR, k)
+            relay_near(k)
+            if n < 4:
+                relay_back(n + 4)
+            if n >= 1:
+                sums(OWN, 2 * n - 2, 2 * n - 1)
+        for k in relayed:
+            finish(k, 0, 3)
+        for k in range(DIRECT):
+            finish(k, 0, 3, 2)
+
     for k in range(NC):
         ocopy(k).wait()
 
     for g in range(4):
+        for i in range(count(g)):
+            sent(g, i, MATE, PASS)
+            if g != NEAR:
+                sent(g, i, SIDE)
+    sent(NEAR, 1, SIDE)
+
+    @at_end
+    def _():
+        sent(NEAR, 0, SIDE)
         for h in range(2):
-            sent(g, h, MATE, PASS)
-
-    @at_end
+            sent(OWN, h, OUT)
+
+    @at_inner
     def _():
         for h in range(2):
-            sent(OWN, h, OUT, SIDE)
-            sent(NB, h, SIDE)
-            sent(NEAR, h, SIDE)
-        sent(FAR, 0, SIDE)
-
-    @at_inner
-    def _():
-        for h in range(2):
-            sent(OWN, h, OUT, CROSS, SIDE)
-            sent(NB, h, CROSS, SIDE)
+            sent(OWN, h, OUT, CROSS)
+            sent(NB, h, CROSS)
             sent(NEAR, h, OUT)
-            sent(FAR, h, OUT, SIDE)
-        sent(NEAR, 1, SIDE)
+        for i in range(4):
+            sent(FAR, i, OUT)
         sent(OWN, 0, YCROSS)
-        sent(FAR, 1, YOUT)
 
     for k in range(NC):
         for g in range(4):
@@ -480,7 +538,6 @@
 def solution(mesh):
     row_spec = P(('data', 'outer', 'expert'), None)
     weight_spec = P(('outer', 'expert'), None, None)
-    vmem = pl.BlockSpec(memory_space=pltpu.VMEM)
     anyspace = pl.BlockSpec(memory_space=pl.ANY)
     dma = pltpu.SemaphoreType.DMA
 
@@ -489,12 +546,14 @@
             kernel,
             name='moe',
             out_shape=jax.ShapeDtypeStruct((TOK, DIM), BF16),
-            in_specs=[anyspace, anyspace, vmem, anyspace, anyspace, anyspace],
+            in_specs=[anyspace] * 6,
             out_specs=anyspace,
             scratch_shapes=[
                 pltpu.VMEM((2, HT, DIM), BF16),
                 pltpu.VMEM((2, COLS, 2, TOPK, 128), F32),
                 pltpu.VMEM((NEXP, DIM), BF16),
+                pltpu.VMEM((TOPK, TOK), jnp.int32),
+                pltpu.VMEM((JLOC * MR, HT), BF16),
                 pltpu.VMEM((JLOC, MR, DIM), BF16),
                 pltpu.VMEM((JLOC, DIM, FF), BF16),
                 pltpu.VMEM((JLOC, DIM, FF), BF16),
@@ -506,9 +565,9 @@
                 pltpu.VMEM((NC, 4, TOK, CW), F32),
                 pltpu.VMEM((NC, 5, TOK, CW), F32),
                 pltpu.VMEM((TOK, DIM), BF16),
-                dma((2,)), dma((2, JLOC)), dma((WSLOT,)), dma((NC,)),
-                dma((7, 4, 2)), dma((7, 4)),
-                dma((COLS, PLANES, 2)), dma((COLS, PLANES)),
+                dma((3,)), dma((2, JLOC)), dma((WSLOT,)), dma((NC,)),
+                dma((6, 4, 4)), dma((6, 4)),
+                dma((COLS, PLANES, 4)), dma((COLS, PLANES)),
                 dma((4, NC, COLS - 1)), dma((4, NC, COLS - 1)),
                 dma((NC, 4)), dma((NC, 5)),
             ],

time: 78.6 us -> 78 us (level)
  the two profiles are of different devices: /device:TPU:8 before, /device:TPU:10 now
where the time goes in v5:
time: 78 us; the launch traced here: 77.8 us
  Pallas kernels  76.1 us (98%)
  local copies, waits for them, and re-layouts  1.67 us (2%)
    pallas_call x1, Pallas kernels, per_device(): pl.pallas_call(kernel, name='moe', out_shape=jax.ShapeDtypeStruct((TOK, D...  76.1 us
    unnamed x1, local copies, waits for them, and re-layouts  1.67 us

profile of v5, /device:TPU:10, one launch (start us, length us, event | category | flops | bytes accessed | tf_op | source)
XLA Modules:
  0.0 77.8 jit_solution(2753028311299539184)
XLA Ops:
  0.0 76.1 %moe.1 = bf16[64,2048]{1,0:T(8,128)(2,1)} custom-call(bf16[64,2048]{1,0:T(8,128)(2,1)} %x_hbm.1, bf16[64,2048]{1,0:T(8,128)(2,1)} %bitcast.2, s32[8,64]{1,0:T(8,128)} %bitcast.3, bf16[4,2048,1024]{2,1,0:T(8,128)(2,1)} %wg_hbm.1, bf16[4,2048,1024]{2,1,0:T(8,128)(2,1)} %wu_hbm.1, bf16[4,1024,2048]{2,1,0:T(8,128)(2,1)} %wd_hbm.1), custom_call_target="tpu_custom_call" | custom-call | tf_op jit(solution)/shard_map/moe/pallas_call | solution.py:545
  76.2 1.7 %copy.8 = bf16[64,2048]{1,0:T(8,128)(2,1)} copy(bf16[64,2048]{1,0:T(8,128)(2,1)} %moe.1) | data formatting | bytes 524288

commit v6 on v5

--- a/solution.py
+++ b/solution.py
@@ -26,7 +26,8 @@
 CT = 2 * TOK
 HT = COLS * CT
 NB, OWN, FAR, NEAR = range(4)
-OUT, CROSS, SIDE, MATE, PASS, YCROSS = range(6)
+OUT, CROSS, SIDE, MATE, PASS, YCROSS, YOUT = range(7)
+ZPART = {NB: 0, FAR: 1, NEAR: 2, OWN: 3}
 
 
 def iota(shape, dim):
@@ -43,7 +44,7 @@
 
 def kernel(x_hbm, wr_hbm, rt_hbm, wg_hbm, wu_hbm, wd_hbm, out_hbm,
            x_all, r_all, wr, rt, sel, xs, wgb, wub, wdb, hid, ysend, yrecv, wst, part, zr, obuf,
-           lsem, wsem, dsem, osem, bx_s, br_s, bx_r, br_r, ys_s, ys_r, zs_s, zs_r):
+           lsem, wsem, dsem, osem, bx_s, br_s, bx_r, br_r, mx_r, mr_r, ys_s, ys_r, zs_s, zs_r):
     d = lax.axis_index('data')
     o = lax.axis_index('outer')
     e = lax.axis_index('expert')
@@ -129,57 +130,66 @@
     def count(g, direction=MATE):
         return 4 if g == FAR or (g, direction) == (NB, CROSS) else 2
 
-    def block(col, g, i, n, direction, oo, ee):
+    targets = {OUT: (e, nbp, e), CROSS: (e, other, e), SIDE: (e, o, yp), MATE: (e, o, mate),
+               PASS: (yp, o, mate), YCROSS: (yp, other, e), YOUT: (yp, nbp, e)}
+
+    def block(g, i, n, direction):
+        col, oo, ee = targets[direction]
         half, rows = rows_of(col, g, i, n)
+        if direction in (MATE, PASS):
+            x_sem, r_sem = mx_r.at[planes[g] // 2], mr_r.at[planes[g] // 2]
+        else:
+            lane = 0 if direction in (OUT, CROSS) else 1
+            x_sem, r_sem = bx_r.at[lane, planes[g], i], br_r.at[lane, planes[g]]
         cps = [pltpu.make_async_remote_copy(
             src_ref=x_all.at[half, rows], dst_ref=x_all.at[half, rows],
-            send_sem=bx_s.at[direction, g, i], recv_sem=bx_r.at[col, planes[g], i],
+            send_sem=bx_s.at[direction], recv_sem=x_sem,
             device_id=(d, oo, ee), device_id_type=MESH)]
         if i == 0:
             tile = r_all.at[half, col, planes[g] % 2]
             cps.insert(0, pltpu.make_async_remote_copy(
                 src_ref=tile, dst_ref=tile,
-                send_sem=br_s.at[direction, g], recv_sem=br_r.at[col, planes[g]],
+                send_sem=br_s.at[direction], recv_sem=r_sem,
                 device_id=(d, oo, ee), device_id_type=MESH))
         return cps
 
-    targets = {OUT: (e, nbp, e), CROSS: (e, other, e), SIDE: (e, o, yp), MATE: (e, o, mate),
-               PASS: (yp, o, mate), YCROSS: (yp, other, e)}
-
-    def pieces(g, i, direction):
-        n, base = count(g, direction), count(g)
-        return n, range(i * n // base, (i + 1) * n // base)
-
     def send(g, i, *directions):
         for direction in directions:
-            col, oo, ee = targets[direction]
-            n, parts = pieces(g, i, direction)
-            for k in parts:
-                for cp in block(col, g, k, n, direction, oo, ee):
+            n, base = count(g, direction), count(g)
+            for k in range(i * n // base, (i + 1) * n // base):
+                for cp in block(g, k, n, direction):
                     cp.start()
 
-    def arrive(col, g, i):
-        for cp in block(col, g, i, count(g), MATE, o, mate):
-            cp.wait_recv()
-
-    def sent(g, i, *directions):
-        for direction in directions:
-            n, parts = pieces(g, i, direction)
-            for k in parts:
-                for cp in block(targets[direction][0], g, k, n, direction, o, mate):
-                    cp.wait_send()
+    def arrive(lane, g, i):
+        n = count(g)
+        half, rows = rows_of((e, yp)[lane], g, i, n)
+        piece = x_all.at[half, rows]
+        if i == 0:
+            tile = r_all.at[half, (e, yp)[lane], planes[g] % 2]
+            pltpu.make_async_copy(tile, tile, br_r.at[lane, planes[g]]).wait()
+        pltpu.make_async_copy(piece, piece, bx_r.at[lane, planes[g], i]).wait()
+
+    def sent(direction, nrows, ntiles):
+        rows = x_all.at[0, pl.ds(0, nrows)]
+        pltpu.make_async_copy(rows, rows, bx_s.at[direction]).wait()
+        tiles = r_all.at[0, pl.ds(0, ntiles), 0]
+        pltpu.make_async_copy(tiles, tiles, br_s.at[direction]).wait()
 
     def get(g, i, *directions):
-        arrive(e, g, i)
+        arrive(0, g, i)
         send(g, i, *directions, MATE)
 
     def yget(g, i, *directions):
-        arrive(yp, g, i)
+        arrive(1, g, i)
         send(g, i, *directions, PASS)
 
-    def from_mate(g, i):
-        arrive(mate, g, i)
-        arrive(diag, g, i)
+    def routes_from_mate(ps):
+        tiles = r_all.at[halves[ps], pl.ds(0, 2)]
+        pltpu.make_async_copy(tiles, tiles, mr_r.at[halves[ps]]).wait()
+
+    def rows_from_mate(ps):
+        rows = x_all.at[halves[ps], pl.ds(0, 2 * CT)]
+        pltpu.make_async_copy(rows, rows, mx_r.at[halves[ps]]).wait()
 
     def early_blocks():
         @at_end
@@ -203,8 +213,8 @@
             send(OWN, 0, YCROSS)
             get(NEAR, 1, OUT, SIDE)
             yget(OWN, 1)
-            get(FAR, 0, OUT, SIDE)
-            get(FAR, 1, OUT, SIDE)
+            get(FAR, 0, OUT)
+            get(FAR, 1, OUT)
             yget(NB, 0)
 
     def mid_blocks():
@@ -217,17 +227,22 @@
         def _():
             get(FAR, 2, OUT, SIDE)
             get(FAR, 3, OUT, SIDE)
+            send(FAR, 0, SIDE)
+            send(FAR, 1, SIDE)
             yget(NB, 1)
 
     zlate = ([(FAR, 0)], [(FAR, 1)], [(FAR, 2)], [(FAR, 3)], [], [], [], [])
     ylate_end = ([], [(NEAR, 0)], [], [(NEAR, 1)], [(FAR, 0)], [(FAR, 1)], [(FAR, 2)], [(FAR, 3)])
-    ylate_inner = ([(NEAR, 0)], [(NEAR, 1)], [(FAR, 0), (FAR, 1)], [(FAR, 2)], [(FAR, 3)], [], [], [])
+    ylate_inner = ([(NEAR, 0)], [(NEAR, 1), (FAR, 2)], [(FAR, 3)], [(FAR, 0)], [(FAR, 1)], [], [], [])
 
     def late_blocks(step):
         @at_end
         def _():
             for g, i in zlate[step]:
-                get(g, i, SIDE)
+                if i < 2:
+                    get(g, i, SIDE)
+                else:
+                    get(g, i)
             for g, i in ylate_end[step]:
                 yget(g, i)
 
@@ -235,7 +250,10 @@
             @at_inner
             def _():
                 for g, i in ylate_inner[step]:
-                    yget(g, i)
+                    if g == FAR and i >= 2:
+                        yget(g, i, YOUT)
+                    else:
+                        yget(g, i)
 
     col_i, row_i = iota((CT, CT), 1), iota((CT, CT), 0)
     same = col_i // TOK == row_i // TOK
@@ -319,8 +337,12 @@
     def ycopy(g, k, q):
         return pltpu.make_async_remote_copy(
             src_ref=ysend.at[g, k, q - 1], dst_ref=yrecv.at[g, k, q],
-            send_sem=ys_s.at[g, k, q - 1], recv_sem=ys_r.at[g, k, q - 1],
+            send_sem=ys_s, recv_sem=ys_r.at[g, k],
             device_id=(d, o, rel[q]), device_id_type=MESH)
+
+    def ywait(g, k):
+        rows = yrecv.at[g, k, pl.ds(1, COLS - 1)]
+        pltpu.make_async_copy(rows, rows, ys_r.at[g, k]).wait()
 
     def ystart(g, k):
         for q in (2, 3, 1):
@@ -346,24 +368,27 @@
 
     def zcopy(k, g, slot, oo):
         return pltpu.make_async_remote_copy(
-            src_ref=part.at[k, g], dst_ref=zr.at[k, slot],
-            send_sem=zs_s.at[k, g], recv_sem=zs_r.at[k, slot],
+            src_ref=part.at[ZPART[g], k], dst_ref=zr.at[k, slot],
+            send_sem=zs_s, recv_sem=zs_r.at[k, slot],
             device_id=(d, oo, e), device_id_type=MESH)
+
+    def zwait(k, slot):
+        rows = zr.at[k, slot]
+        pltpu.make_async_copy(rows, rows, zs_r.at[k, slot]).wait()
 
     def sums(g, *chunks):
         for k in chunks:
-            for q in range(1, COLS):
-                ycopy(g, k, q).wait_recv()
+            ywait(g, k)
         for k in chunks:
             acc = dot(wst[g], yrecv[g, k].reshape(SW, CW))
-            part[k, g] = acc[0:TOK] + acc[TOK:2 * TOK] + acc[2 * TOK:3 * TOK]
+            part[ZPART[g], k] = acc[0:TOK] + acc[TOK:2 * TOK] + acc[2 * TOK:3 * TOK]
 
     def zsend(k, g, slot, oo):
         zcopy(k, g, slot, oo).start()
 
     def relay(k, g, slot_in, slot_out, oo):
-        zcopy(k, g, slot_in, nbp).wait_recv()
-        part[k, g] = part[k, g] + zr[k, slot_in]
+        zwait(k, slot_in)
+        part[ZPART[g], k] = part[ZPART[g], k] + zr[k, slot_in]
         zcopy(k, g, slot_out, oo).start()
 
     def relay_far(k):
@@ -377,14 +402,13 @@
 
     def ocopy(k):
         cols = pl.ds(k * CW, CW)
-        return pltpu.make_async_copy(obuf.at[:, cols], out_hbm.at[:, cols], osem.at[k])
+        return pltpu.make_async_copy(obuf.at[:, cols], out_hbm.at[:, cols], osem)
 
     def finish(k, *slots):
         cols = pl.ds(k * CW, CW)
-        total = None
         for slot in slots:
-            zcopy(k, OWN, slot, nbp).wait_recv()
-        total = part[k, OWN]
+            zwait(k, slot)
+        total = part[ZPART[OWN], k]
         for slot in slots:
             total = total + zr[k, slot]
         obuf[:, cols] = total.astype(BF16)
@@ -393,12 +417,10 @@
     early_blocks()
     wrcp.wait()
     gates(0)
-    from_mate(OWN, 0)
-    from_mate(NB, 0)
+    routes_from_mate(0)
     choose(0)
     mid_blocks()
-    from_mate(OWN, 1)
-    from_mate(NB, 1)
+    rows_from_mate(0)
     pick(0)
     for j in range(JLOC):
         gate_up(0, j)
@@ -416,13 +438,10 @@
             for k in chunks:
                 zsend(k, NB, 0, nbp)
 
-    from_mate(NEAR, 0)
-    from_mate(NEAR, 1)
-    from_mate(FAR, 0)
+    routes_from_mate(1)
     choose(1)
     sums_nb(0, 1)
-    for i in range(1, 4):
-        from_mate(FAR, i)
+    rows_from_mate(1)
     pick(1)
     for j in range(JLOC):
         gate_up(1, j)
@@ -501,38 +520,28 @@
         for k in range(DIRECT):
             finish(k, 0, 3, 2)
 
-    for k in range(NC):
-        ocopy(k).wait()
-
-    for g in range(4):
-        for i in range(count(g)):
-            sent(g, i, MATE, PASS)
-            if g != NEAR:
-                sent(g, i, SIDE)
-    sent(NEAR, 1, SIDE)
+    pltpu.make_async_copy(obuf, out_hbm, osem).wait()
+
+    sent(MATE, 4 * TOK, 4)
+    sent(PASS, 4 * TOK, 4)
 
     @at_end
     def _():
-        sent(NEAR, 0, SIDE)
-        for h in range(2):
-            sent(OWN, h, OUT)
+        sent(SIDE, 7 * TOK // 2, 4)
+        sent(OUT, TOK, 1)
 
     @at_inner
     def _():
-        for h in range(2):
-            sent(OWN, h, OUT, CROSS)
-            sent(NB, h, CROSS)
-            sent(NEAR, h, OUT)
-        for i in range(4):
-            sent(FAR, i, OUT)
-        sent(OWN, 0, YCROSS)
-
-    for k in range(NC):
-        for g in range(4):
-            for q in range(1, COLS):
-                ycopy(g, k, q).wait_send()
-            if g != OWN:
-                zcopy(k, g, 0, nbp).wait_send()
+        sent(SIDE, 7 * TOK // 2, 3)
+        sent(OUT, 3 * TOK, 3)
+        sent(CROSS, 2 * TOK, 2)
+        sent(YCROSS, TOK // 2, 1)
+        half_rows = x_all.at[0, pl.ds(0, TOK // 2)]
+        pltpu.make_async_copy(half_rows, half_rows, bx_s.at[YOUT]).wait()
+
+    pltpu.make_async_copy(ysend, ysend, ys_s).wait()
+    moved = part.at[pl.ds(0, 3)]
+    pltpu.make_async_copy(moved, moved, zs_s).wait()
 
 
 def solution(mesh):
@@ -562,14 +571,13 @@
                 pltpu.VMEM((4, NC, COLS - 1, GR, CW), BF16),
                 pltpu.VMEM((4, NC, COLS, GR, CW), BF16),
                 pltpu.VMEM((4, 3 * TOK, SW), BF16),
-                pltpu.VMEM((NC, 4, TOK, CW), F32),
+                pltpu.VMEM((4, NC, TOK, CW), F32),
                 pltpu.VMEM((NC, 5, TOK, CW), F32),
                 pltpu.VMEM((TOK, DIM), BF16),
-                dma((3,)), dma((2, JLOC)), dma((WSLOT,)), dma((NC,)),
-                dma((6, 4, 4)), dma((6, 4)),
-                dma((COLS, PLANES, 4)), dma((COLS, PLANES)),
-                dma((4, NC, COLS - 1)), dma((4, NC, COLS - 1)),
-                dma((NC, 4)), dma((NC, 5)),
+                dma((3,)), dma((2, JLOC)), dma((WSLOT,)), dma,
+                dma((7,)), dma((7,)),
+                dma((2, PLANES, 4)), dma((2, PLANES)), dma((2,)), dma((2,)),
+                dma, dma((4, NC)), dma, dma((NC, 5)),
             ],
             compiler_params=pltpu.CompilerParams(
                 collective_id=0, has_side_effects=True, vmem_limit_bytes=67043328),

time: 78 us -> 74.6 us (0.956)
  the two profiles are of different devices: /device:TPU:10 before, /device:TPU:11 now
where the time goes in v6:
time: 74.6 us; the launch traced here: 74.4 us
  Pallas kernels  72.8 us (98%)
  local copies, waits for them, and re-layouts  1.67 us (2%)
    pallas_call x1, Pallas kernels, per_device(): pl.pallas_call(kernel, name='moe', out_shape=jax.ShapeDtypeStruct((TOK, D...  72.8 us
    unnamed x1, local copies, waits for them, and re-layouts  1.67 us

profile of v6, /device:TPU:11, one launch (start us, length us, event | category | flops | bytes accessed | tf_op | source)
XLA Modules:
  0.0 74.4 jit_solution(9163948331573090642)
XLA Ops:
  0.0 72.8 %moe.1 = bf16[64,2048]{1,0:T(8,128)(2,1)} custom-call(bf16[64,2048]{1,0:T(8,128)(2,1)} %x_hbm.1, bf16[64,2048]{1,0:T(8,128)(2,1)} %bitcast.2, s32[8,64]{1,0:T(8,128)} %bitcast.3, bf16[4,2048,1024]{2,1,0:T(8,128)(2,1)} %wg_hbm.1, bf16[4,2048,1024]{2,1,0:T(8,128)(2,1)} %wu_hbm.1, bf16[4,1024,2048]{2,1,0:T(8,128)(2,1)} %wd_hbm.1), custom_call_target="tpu_custom_call" | custom-call | tf_op jit(solution)/shard_map/moe/pallas_call | solution.py:554
  72.8 1.7 %copy.8 = bf16[64,2048]{1,0:T(8,128)(2,1)} copy(bf16[64,2048]{1,0:T(8,128)(2,1)} %moe.1) | data formatting | bytes 524288

commit v7 on v6

--- a/solution.py
+++ b/solution.py
@@ -42,9 +42,9 @@
     return lax.dot_general(a, b, (((1,), (1,)), ((), ())), preferred_element_type=F32)
 
 
-def kernel(x_hbm, wr_hbm, rt_hbm, wg_hbm, wu_hbm, wd_hbm, out_hbm,
-           x_all, r_all, wr, rt, sel, xs, wgb, wub, wdb, hid, ysend, yrecv, wst, part, zr, obuf,
-           lsem, wsem, dsem, osem, bx_s, br_s, bx_r, br_r, mx_r, mr_r, ys_s, ys_r, zs_s, zs_r):
+def kernel(x_hbm, wr_hbm, rt_hbm, wg_hbm, wu_hbm, wd_hbm, out_ref,
+           x_all, r_all, wr, rt, sel, xs, wgb, wub, wdb, hid, ysend, yrecv, wst, part, zr,
+           lsem, wsem, dsem, bx_s, br_s, bx_r, br_r, mx_r, mr_r, ys_s, ys_r, zs_s, zs_r):
     d = lax.axis_index('data')
     o = lax.axis_index('outer')
     e = lax.axis_index('expert')
@@ -400,10 +400,6 @@
     def relay_back(k):
         relay(k, NB, 4, 0, nbp)
 
-    def ocopy(k):
-        cols = pl.ds(k * CW, CW)
-        return pltpu.make_async_copy(obuf.at[:, cols], out_hbm.at[:, cols], osem)
-
     def finish(k, *slots):
         cols = pl.ds(k * CW, CW)
         for slot in slots:
@@ -411,8 +407,7 @@
         total = part[ZPART[OWN], k]
         for slot in slots:
             total = total + zr[k, slot]
-        obuf[:, cols] = total.astype(BF16)
-        ocopy(k).start()
+        out_ref[:, cols] = total.astype(BF16)
 
     early_blocks()
     wrcp.wait()
@@ -440,13 +435,12 @@
 
     routes_from_mate(1)
     choose(1)
-    sums_nb(0, 1)
     rows_from_mate(1)
     pick(1)
     for j in range(JLOC):
         gate_up(1, j)
         if j < JLOC - 1:
-            sums_nb(2 * j + 2, 2 * j + 3)
+            sums_nb(2 * j, 2 * j + 1)
 
     def sums_far(k):
         sums(FAR, k)
@@ -492,6 +486,9 @@
         for k in range(DIRECT):
             sums(NEAR, k)
             zsend(k, NEAR, 2, planes[NEAR])
+        sums(NB, NC - 2, NC - 1)
+        for k in (NC - 2, NC - 1):
+            zsend(k, NB, 0, nbp)
         for k in range(0, NC, 2):
             sums(OWN, k, k + 1)
         for k in range(NC):
@@ -506,6 +503,8 @@
         for k in range(NC):
             sums(FAR, k)
             relay_far(k)
+            if k == 0:
+                sums(NB, NC - 2, NC - 1)
             if k >= 4:
                 relay_back(k - 4)
         for n, k in enumerate(relayed):
@@ -515,12 +514,13 @@
                 relay_back(n + 4)
             if n >= 1:
                 sums(OWN, 2 * n - 2, 2 * n - 1)
-        for k in relayed:
+        for k in relayed[:-2]:
             finish(k, 0, 3)
         for k in range(DIRECT):
             finish(k, 0, 3, 2)
-
-    pltpu.make_async_copy(obuf, out_hbm, osem).wait()
+        for k in relayed[-2:]:
+            finish(k, 0, 3)
+
 
     sent(MATE, 4 * TOK, 4)
     sent(PASS, 4 * TOK, 4)
@@ -554,9 +554,9 @@
         return pl.pallas_call(
             kernel,
             name='moe',
-            out_shape=jax.ShapeDtypeStruct((TOK, DIM), BF16),
+            out_shape=pltpu.VMEM((TOK, DIM), BF16),
             in_specs=[anyspace] * 6,
-            out_specs=anyspace,
+            out_specs=pl.BlockSpec(memory_space=pltpu.VMEM),
             scratch_shapes=[
                 pltpu.VMEM((2, HT, DIM), BF16),
                 pltpu.VMEM((2, COLS, 2, TOPK, 128), F32),
@@ -573,14 +573,13 @@
                 pltpu.VMEM((4, 3 * TOK, SW), BF16),
                 pltpu.VMEM((4, NC, TOK, CW), F32),
                 pltpu.VMEM((NC, 5, TOK, CW), F32),
-                pltpu.VMEM((TOK, DIM), BF16),
-                dma((3,)), dma((2, JLOC)), dma((WSLOT,)), dma,
+                dma((3,)), dma((2, JLOC)), dma((WSLOT,)),
                 dma((7,)), dma((7,)),
                 dma((2, PLANES, 4)), dma((2, PLANES)), dma((2,)), dma((2,)),
                 dma, dma((4, NC)), dma, dma((NC, 5)),
             ],
             compiler_params=pltpu.CompilerParams(
-                collective_id=0, has_side_effects=True, vmem_limit_bytes=67043328),
+                collective_id=0, has_side_effects=True, vmem_limit_bytes=67043328 - (1 << 20)),
         )(tokens, w_router.T, routes.T, w_gate, w_up, w_down)
 
     return jax.shard_map(

time: 74.6 us -> 72.9 us (0.977)
  the two profiles are of different devices: /device:TPU:11 before, /device:TPU:0 now
where the time goes in v7:
time: 72.9 us; the launch traced here: 72.1 us
  Pallas kernels  71.4 us (98%)
    pallas_call x1, Pallas kernels, per_device(): pl.pallas_call(kernel, name='moe', out_shape=pltpu.VMEM((TOK, DIM), BF16)...  71.4 us

profile of v7, /device:TPU:0, one launch (start us, length us, event | category | flops | bytes accessed | tf_op | source)
XLA Modules:
  0.0 72.1 jit_solution(4749862568223873495)
XLA Ops:
  0.0 71.4 %moe.1 = bf16[64,2048]{1,0:T(8,128)(2,1)S(1)} custom-call(bf16[64,2048]{1,0:T(8,128)(2,1)} %x_hbm.1, bf16[64,2048]{1,0:T(8,128)(2,1)} %bitcast.2, s32[8,64]{1,0:T(8,128)} %bitcast.3, bf16[4,2048,1024]{2,1,0:T(8,128)(2,1)} %wg_hbm.1, bf16[4,2048,1024]{2,1,0:T(8,128)(2,1)} %wu_hbm.1, bf16[4,1024,2048]{2,1,0:T(8,128)(2,1)} %wd_hbm.1), custom_call_target="tpu_custom_call" | custom-call | tf_op jit(solution)/shard_map/moe/pallas_call | solution.py:554
  71.4 0.7 copy.8

commit v8 on v7

--- a/solution.py
+++ b/solution.py
@@ -44,7 +44,7 @@
 
 def kernel(x_hbm, wr_hbm, rt_hbm, wg_hbm, wu_hbm, wd_hbm, out_ref,
            x_all, r_all, wr, rt, sel, xs, wgb, wub, wdb, hid, ysend, yrecv, wst, part, zr,
-           lsem, wsem, dsem, bx_s, br_s, bx_r, br_r, mx_r, mr_r, ys_s, ys_r, zs_s, zs_r):
+           lsem, wsem, dsem, bx_s, br_s, bx_r, br_r, mx_r, mr_r, ys_s, ys_r, zs_s, zs_r, zh_r):
     d = lax.axis_index('data')
     o = lax.axis_index('outer')
     e = lax.axis_index('expert')
@@ -376,6 +376,17 @@
         rows = zr.at[k, slot]
         pltpu.make_async_copy(rows, rows, zs_r.at[k, slot]).wait()
 
+    def half_copy(i, slot, oo):
+        cols = pl.ds(i * (CW // 2), CW // 2)
+        sem = zs_r.at[0, slot] if i == 0 else zh_r.at[slot // 4]
+        return pltpu.make_async_remote_copy(
+            src_ref=part.at[ZPART[FAR], 0, :, cols], dst_ref=zr.at[0, slot, :, cols],
+            send_sem=zs_s, recv_sem=sem, device_id=(d, oo, e), device_id_type=MESH)
+
+    def half_wait(i, slot):
+        rows = zr.at[0, slot, :, pl.ds(i * (CW // 2), CW // 2)]
+        pltpu.make_async_copy(rows, rows, zs_r.at[0, slot] if i == 0 else zh_r.at[slot // 4]).wait()
+
     def sums(g, *chunks):
         for k in chunks:
             ywait(g, k)
@@ -392,13 +403,26 @@
         zcopy(k, g, slot_out, oo).start()
 
     def relay_far(k):
-        relay(k, FAR, 1, 4, other)
+        if k:
+            relay(k, FAR, 1, 4, other)
+            return
+        for i in range(2):
+            cols = pl.ds(i * (CW // 2), CW // 2)
+            half_wait(i, 1)
+            part[ZPART[FAR], 0, :, cols] = part[ZPART[FAR], 0, :, cols] + zr[0, 1, :, cols]
+            half_copy(i, 4, other).start()
 
     def relay_near(k):
         relay(k, NEAR, 2, 3, other)
 
     def relay_back(k):
-        relay(k, NB, 4, 0, nbp)
+        if k:
+            relay(k, NB, 4, 0, nbp)
+            return
+        for i in range(2):
+            half_wait(i, 4)
+        part[ZPART[NB], 0] = part[ZPART[NB], 0] + zr[0, 4]
+        zcopy(0, NB, 0, nbp).start()
 
     def finish(k, *slots):
         cols = pl.ds(k * CW, CW)
@@ -422,8 +446,8 @@
         late_blocks(j)
     for k in range(NC):
         down_chunk(0, k)
-        if k % 2:
-            late_blocks(JLOC + k // 2)
+        for step in {0: (4,), 2: (5,), 3: (6,), 5: (7,)}.get(k, ()):
+            late_blocks(step)
 
     def sums_nb(*chunks):
         sums(NB, *chunks)
@@ -444,7 +468,11 @@
 
     def sums_far(k):
         sums(FAR, k)
-        zsend(k, FAR, 1, nbp)
+        if k:
+            zsend(k, FAR, 1, nbp)
+        else:
+            for i in range(2):
+                half_copy(i, 1, nbp).start()
 
     lead = 4
     relayed = tuple(range(DIRECT, NC))
@@ -576,7 +604,7 @@
                 dma((3,)), dma((2, JLOC)), dma((WSLOT,)),
                 dma((7,)), dma((7,)),
                 dma((2, PLANES, 4)), dma((2, PLANES)), dma((2,)), dma((2,)),
-                dma, dma((4, NC)), dma, dma((NC, 5)),
+                dma, dma((4, NC)), dma, dma((NC, 5)), dma((2,)),
             ],
             compiler_params=pltpu.CompilerParams(
                 collective_id=0, has_side_effects=True, vmem_limit_bytes=67043328 - (1 << 20)),

time: 72.9 us -> 72 us (0.988)
  no operation moved by 1% of the time
where the time goes in v8:
time: 72 us; the launch traced here: 71.6 us
  Pallas kernels  70.8 us (98%)
    pallas_call x1, Pallas kernels, per_device(): pl.pallas_call(kernel, name='moe', out_shape=pltpu.VMEM((TOK, DIM), BF16)...  70.8 us

profile of v8, /device:TPU:0, one launch (start us, length us, event | category | flops | bytes accessed | tf_op | source)
XLA Modules:
  0.0 71.6 jit_solution(1601967558717174902)
XLA Ops:
  0.0 70.8 %moe.1 = bf16[64,2048]{1,0:T(8,128)(2,1)S(1)} custom-call(bf16[64,2048]{1,0:T(8,128)(2,1)} %x_hbm.1, bf16[64,2048]{1,0:T(8,128)(2,1)} %bitcast.2, s32[8,64]{1,0:T(8,128)} %bitcast.3, bf16[4,2048,1024]{2,1,0:T(8,128)(2,1)} %wg_hbm.1, bf16[4,2048,1024]{2,1,0:T(8,128)(2,1)} %wu_hbm.1, bf16[4,1024,2048]{2,1,0:T(8,128)(2,1)} %wd_hbm.1), custom_call_target="tpu_custom_call" | custom-call | tf_op jit(solution)/shard_map/moe/pallas_call | solution.py:582
  70.8 0.7 copy.8

commit v9 on v8

--- a/solution.py
+++ b/solution.py
@@ -20,6 +20,7 @@
 NC = DIM // CW
 DIRECT = 3
 WSLOT = 6
+EARLY = 6
 GR = JLOC * CAP
 MR = 2 * COLS * CAP
 SW = COLS * GR
@@ -114,7 +115,7 @@
 
     def wd_copy(n):
         return pltpu.make_async_copy(
-            wd_hbm.at[:, :, pl.ds((n % NC) * CW, CW)], wdb.at[n % WSLOT], dsem.at[n % WSLOT])
+            wd_hbm.at[:, :, pl.ds((n if n < EARLY else n - EARLY) * CW, CW)], wdb.at[n % WSLOT], dsem.at[n % WSLOT])
 
     for n in range(WSLOT):
         wd_copy(n).start()
@@ -332,7 +333,7 @@
             cols = slice(n * 512, (n + 1) * 512)
             ga = dot(xs[j], wgb[j, :, cols])
             gu = dot(xs[j], wub[j, :, cols])
-            hid[j, :, cols] = (jax.nn.silu(ga) * gu).astype(BF16)
+            hid[j, ps * MR:(ps + 1) * MR, cols] = (jax.nn.silu(ga) * gu).astype(BF16)
 
     def ycopy(g, k, q):
         return pltpu.make_async_remote_copy(
@@ -349,21 +350,24 @@
             ycopy(g, k, q).start()
 
     def down_chunk(ps, k):
-        n = ps * NC + k
+        n = k if ps == 0 else EARLY + k
+        both = ps == 1 and k >= EARLY
+        first = 0 if both else ps * MR
         wd_copy(n).wait()
-        outs = [dot(hid[j], wdb[n % WSLOT, j]) for j in range(JLOC)]
-        for i in range(2):
-            g = 2 * ps + i
-            for q in (2, 3, 1, 0):
-                at = i * GR + q * CAP
-                rows = jnp.concatenate([r[at:at + CAP] for r in outs], axis=0).astype(BF16)
-                if q:
-                    ysend[g, k, q - 1] = rows
-                else:
-                    yrecv[g, k, 0] = rows
+        outs = [dot(hid[j, first:(ps + 1) * MR], wdb[n % WSLOT, j]) for j in range(JLOC)]
+        for pp in ((1, 0) if both else (ps,)):
+            for i in range(2):
+                g = 2 * pp + i
+                for q in (2, 3, 1, 0):
+                    at = pp * MR - first + i * GR + q * CAP
+                    rows = jnp.concatenate([r[at:at + CAP] for r in outs], axis=0).astype(BF16)
+                    if q:
+                        ysend[g, k, q - 1] = rows
+                    else:
+                        yrecv[g, k, 0] = rows
         if ps == 0:
             ystart(NB, k)
-        if n + WSLOT < 2 * NC:
+        if n + WSLOT < EARLY + NC:
             wd_copy(n + WSLOT).start()
 
     def zcopy(k, g, slot, oo):
@@ -444,9 +448,9 @@
     for j in range(JLOC):
         gate_up(0, j)
         late_blocks(j)
-    for k in range(NC):
+    for k in range(EARLY):
         down_chunk(0, k)
-        for step in {0: (4,), 2: (5,), 3: (6,), 5: (7,)}.get(k, ()):
+        for step in {0: (4, 5), 1: (6,), 3: (7,)}.get(k, ()):
             late_blocks(step)
 
     def sums_nb(*chunks):
@@ -504,6 +508,8 @@
     def _():
         for k in relayed + tuple(range(DIRECT)):
             ystart(NEAR, k)
+        for k in range(EARLY, NC):
+            ystart(NB, k)
         for k in range(NC):
             ystart(OWN, k)
         for k in range(lead, NC):
@@ -526,13 +532,13 @@
     def _():
         for k in relayed:
             ystart(NEAR, k)
+        for k in range(EARLY, NC):
+            ystart(NB, k)
         for k in range(NC):
             ystart(OWN, k)
         for k in range(NC):
             sums(FAR, k)
             relay_far(k)
-            if k == 0:
-                sums(NB, NC - 2, NC - 1)
             if k >= 4:
                 relay_back(k - 4)
         for n, k in enumerate(relayed):
@@ -540,8 +546,11 @@
             relay_near(k)
             if n < 4:
                 relay_back(n + 4)
-            if n >= 1:
-                sums(OWN, 2 * n - 2, 2 * n - 1)
+            if n == 1:
+                sums(NB, NC - 2, NC - 1)
+            if n >= 2:
+                sums(OWN, 2 * n - 4, 2 * n - 3)
+        sums(OWN, NC - 2, NC - 1)
         for k in relayed[:-2]:
             finish(k, 0, 3)
         for k in range(DIRECT):
@@ -595,7 +604,7 @@
                 pltpu.VMEM((JLOC, DIM, FF), BF16),
                 pltpu.VMEM((JLOC, DIM, FF), BF16),
                 pltpu.VMEM((WSLOT, JLOC, FF, CW), BF16),
-                pltpu.VMEM((JLOC, MR, FF), BF16),
+                pltpu.VMEM((JLOC, 2 * MR, FF), BF16),
                 pltpu.VMEM((4, NC, COLS - 1, GR, CW), BF16),
                 pltpu.VMEM((4, NC, COLS, GR, CW), BF16),
                 pltpu.VMEM((4, 3 * TOK, SW), BF16),

time: 72 us -> 71 us (0.986)
  Pallas kernels: 70.8 us -> 69.9 us
    pallas_call x1, Pallas kernels: 70.8 us -> 69.9 us  [per_device(): pl.pallas_call(kernel, name='moe', out_shape=pltpu.VMEM((TOK, DIM), BF16)...]
where the time goes in v9:
time: 71 us; the launch traced here: 70.6 us
  Pallas kernels  69.9 us (98%)
  local copies, waits for them, and re-layouts  0.71 us (1%)
    pallas_call x1, Pallas kernels, per_device(): pl.pallas_call(kernel, name='moe', out_shape=pltpu.VMEM((TOK, DIM), BF16)...  69.9 us

profile of v9, /device:TPU:0, one launch (start us, length us, event | category | flops | bytes accessed | tf_op | source)
XLA Modules:
  0.0 70.6 jit_solution(2466176118103806518)
XLA Ops:
  0.0 69.9 %moe.1 = bf16[64,2048]{1,0:T(8,128)(2,1)S(1)} custom-call(bf16[64,2048]{1,0:T(8,128)(2,1)} %x_hbm.1, bf16[64,2048]{1,0:T(8,128)(2,1)} %bitcast.2, s32[8,64]{1,0:T(8,128)} %bitcast.3, bf16[4,2048,1024]{2,1,0:T(8,128)(2,1)} %wg_hbm.1, bf16[4,2048,1024]{2,1,0:T(8,128)(2,1)} %wu_hbm.1, bf16[4,1024,2048]{2,1,0:T(8,128)(2,1)} %wd_hbm.1), custom_call_target="tpu_custom_call" | custom-call | tf_op jit(solution)/shard_map/moe/pallas_call | solution.py:591
  69.9 0.7 copy.8

commit v10 on v9

--- a/solution.py
+++ b/solution.py
@@ -45,7 +45,7 @@
 
 def kernel(x_hbm, wr_hbm, rt_hbm, wg_hbm, wu_hbm, wd_hbm, out_ref,
            x_all, r_all, wr, rt, sel, xs, wgb, wub, wdb, hid, ysend, yrecv, wst, part, zr,
-           lsem, wsem, dsem, bx_s, br_s, bx_r, br_r, mx_r, mr_r, ys_s, ys_r, zs_s, zs_r, zh_r):
+           lsem, wsem, dsem, bx_s, br_s, bx_r, br_r, mx_r, mr_r, ys_s, ys_r, zs_s, zs_r, zh_r, yh_r):
     d = lax.axis_index('data')
     o = lax.axis_index('outer')
     e = lax.axis_index('expert')
@@ -341,11 +341,31 @@
             send_sem=ys_s, recv_sem=ys_r.at[g, k],
             device_id=(d, o, rel[q]), device_id_type=MESH)
 
+    def half_cols(i):
+        return pl.ds(i * (CW // 2), CW // 2)
+
+    def ywait_half(i):
+        rows = yrecv.at[FAR, 0, pl.ds(1, COLS - 1), :, half_cols(i)]
+        pltpu.make_async_copy(rows, rows, ys_r.at[FAR, 0] if i == 0 else yh_r).wait()
+
     def ywait(g, k):
+        if (g, k) == (FAR, 0):
+            ywait_half(0)
+            ywait_half(1)
+            return
         rows = yrecv.at[g, k, pl.ds(1, COLS - 1)]
         pltpu.make_async_copy(rows, rows, ys_r.at[g, k]).wait()
 
     def ystart(g, k):
+        if (g, k) == (FAR, 0):
+            for i in range(2):
+                for q in (2, 3, 1):
+                    pltpu.make_async_remote_copy(
+                        src_ref=ysend.at[g, k, q - 1, :, half_cols(i)],
+                        dst_ref=yrecv.at[g, k, q, :, half_cols(i)],
+                        send_sem=ys_s, recv_sem=ys_r.at[g, k] if i == 0 else yh_r,
+                        device_id=(d, o, rel[q]), device_id_type=MESH).start()
+            return
         for q in (2, 3, 1):
             ycopy(g, k, q).start()
 
@@ -471,14 +491,18 @@
             sums_nb(2 * j, 2 * j + 1)
 
     def sums_far(k):
-        sums(FAR, k)
         if k:
+            sums(FAR, k)
             zsend(k, FAR, 1, nbp)
-        else:
-            for i in range(2):
-                half_copy(i, 1, nbp).start()
-
-    lead = 4
+            return
+        for i in range(2):
+            ywait_half(i)
+            acc = dot(wst[FAR], yrecv[FAR, 0, :, :, half_cols(i)].reshape(SW, CW // 2))
+            part[ZPART[FAR], 0, :, half_cols(i)] = (
+                acc[0:TOK] + acc[TOK:2 * TOK] + acc[2 * TOK:3 * TOK])
+            half_copy(i, 1, nbp).start()
+
+    lead = 3
     relayed = tuple(range(DIRECT, NC))
     for k in range(NC):
         down_chunk(1, k)
@@ -512,7 +536,7 @@
             ystart(NB, k)
         for k in range(NC):
             ystart(OWN, k)
-        for k in range(lead, NC):
+        for k in range(NC - lead, NC):
             sums_far(k)
         for k in relayed:
             sums(NEAR, k)
@@ -613,7 +637,7 @@
                 dma((3,)), dma((2, JLOC)), dma((WSLOT,)),
                 dma((7,)), dma((7,)),
                 dma((2, PLANES, 4)), dma((2, PLANES)), dma((2,)), dma((2,)),
-                dma, dma((4, NC)), dma, dma((NC, 5)), dma((2,)),
+                dma, dma((4, NC)), dma, dma((NC, 5)), dma((2,)), dma,
             ],
             compiler_params=pltpu.CompilerParams(
                 collective_id=0, has_side_effects=True, vmem_limit_bytes=67043328 - (1 << 20)),

time: 71 us -> 71 us (level)
  no operation moved by 1% of the time
where the time goes in v10:
time: 71 us; the launch traced here: 70.2 us
  Pallas kernels  69.4 us (98%)
  local copies, waits for them, and re-layouts  0.71 us (1%)
    pallas_call x1, Pallas kernels, per_device(): pl.pallas_call(kernel, name='moe', out_shape=pltpu.VMEM((TOK, DIM), BF16)...  69.4 us

profile of v10, /device:TPU:0, one launch (start us, length us, event | category | flops | bytes accessed | tf_op | source)
XLA Modules:
  0.0 70.2 jit_solution(8033151973190185529)
XLA Ops:
  0.0 69.4 %moe.1 = bf16[64,2048]{1,0:T(8,128)(2,1)S(1)} custom-call(bf16[64,2048]{1,0:T(8,128)(2,1)} %x_hbm.1, bf16[64,2048]{1,0:T(8,128)(2,1)} %bitcast.2, s32[8,64]{1,0:T(8,128)} %bitcast.3, bf16[4,2048,1024]{2,1,0:T(8,128)(2,1)} %wg_hbm.1, bf16[4,2048,1024]{2,1,0:T(8,128)(2,1)} %wu_hbm.1, bf16[4,1024,2048]{2,1,0:T(8,128)(2,1)} %wd_hbm.1), custom_call_target="tpu_custom_call" | custom-call | tf_op jit(solution)/shard_map/moe/pallas_call | solution.py:615
  69.5 0.7 %copy.8 = bf16[64,2048]{1,0:T(8,128)(2,1)} copy(bf16[64,2048]{1,0:T(8,128)(2,1)S(1)} %moe.1) | data formatting | bytes 524288

commit v11 on v10

--- a/solution.py
+++ b/solution.py
@@ -18,7 +18,7 @@
 NEXP = 64
 CW = 256
 NC = DIM // CW
-DIRECT = 3
+DIRECT = 2
 WSLOT = 6
 EARLY = 6
 GR = JLOC * CAP
@@ -574,7 +574,8 @@
                 sums(NB, NC - 2, NC - 1)
             if n >= 2:
                 sums(OWN, 2 * n - 4, 2 * n - 3)
-        sums(OWN, NC - 2, NC - 1)
+        for k in range(2 * (len(relayed) - 2), NC, 2):
+            sums(OWN, k, k + 1)
         for k in relayed[:-2]:
             finish(k, 0, 3)
         for k in range(DIRECT):

time: 71 us -> 70.6 us (level)
  no operation moved by 1% of the time
where the time goes in v11:
time: 70.6 us; the launch traced here: 70.2 us
  Pallas kernels  69.4 us (98%)
  local copies, waits for them, and re-layouts  0.71 us (1%)
    pallas_call x1, Pallas kernels, per_device(): pl.pallas_call(kernel, name='moe', out_shape=pltpu.VMEM((TOK, DIM), BF16)...  69.4 us

profile of v11, /device:TPU:0, one launch (start us, length us, event | category | flops | bytes accessed | tf_op | source)
XLA Modules:
  0.0 70.2 jit_solution(12010592901022032564)
XLA Ops:
  0.0 69.4 %moe.1 = bf16[64,2048]{1,0:T(8,128)(2,1)S(1)} custom-call(bf16[64,2048]{1,0:T(8,128)(2,1)} %x_hbm.1, bf16[64,2048]{1,0:T(8,128)(2,1)} %bitcast.2, s32[8,64]{1,0:T(8,128)} %bitcast.3, bf16[4,2048,1024]{2,1,0:T(8,128)(2,1)} %wg_hbm.1, bf16[4,2048,1024]{2,1,0:T(8,128)(2,1)} %wu_hbm.1, bf16[4,1024,2048]{2,1,0:T(8,128)(2,1)} %wd_hbm.1), custom_call_target="tpu_custom_call" | custom-call | tf_op jit(solution)/shard_map/moe/pallas_call | solution.py:616
  69.4 0.7 %copy.8 = bf16[64,2048]{1,0:T(8,128)(2,1)} copy(bf16[64,2048]{1,0:T(8,128)(2,1)S(1)} %moe.1) | data formatting | bytes 524288
